TPU v7x, 256 devices: a whole 4x4x8 slice. The times are simulated.
256 devices in a mesh: lon: 64 (over y_hi, x, z), lat: 4 (over y_lo, core).
Axes of the slice: x: 4, y: 4 (y_hi: 2, y_lo: 2; y = y_hi * 2 + y_lo), z: 8, core: 2. Of those that a mesh axis runs over, the one named last changes fastest.
Arguments:
- increment: bfloat16 [2048, 512, 128], P('lon', 'lat'), may hold values from -6 to 6
- jacobian: bfloat16 [4096, 128, 3072], P(('lon', 'lat')), may hold values from -0.0625 to 0.0625
- lat_weight: float32 [4096, 8], P(('lon', 'lat')), may hold values from 0.2 to 2
- centre: int32 [4096], P(('lon', 'lat')), may hold values from 0 to 31
- west: int32 [4096], P(('lon', 'lat')), may hold values from 0 to 32
- east: int32 [4096], P(('lon', 'lat')), may hold values from 0 to 32
- lat_offset: int32 [4096], P(('lon', 'lat')), may hold values from 0 to 504
- lev_offset: int32 [4096], P(('lon', 'lat')), may hold values from 0 to 96
Outputs:
- departures: float32 [4096, 128], P(('lon', 'lat'))
All inputs are finite; a program needn't handle non-finite values.
Results may differ from a plain program's by a relative error of at most 0.0029.
Values may be sent and summed in bfloat16 or wider, within the bound.
No kernel may reach another device: no remote copies, remote signals or barrier semaphores. Data moves between devices by JAX's collectives and lax.ppermute only.
A program may use at most 128 MiB of HBM per device.

v0:
```python
import jax
import jax.numpy as jnp
from jax import lax
from jax.sharding import PartitionSpec as P

BLAT = 8
BLEV = 32


def padded(block, sides, width):
    for axis, dim in sides:
        count = lax.axis_size(axis)
        forward = [(i, i + 1) for i in range(count - 1)]
        forward.append((count - 1, 0))
        backward = [(target, source) for source, target in forward]
        low = lax.ppermute(
            lax.slice_in_dim(block, block.shape[dim] - width, None, axis=dim), axis, forward
        )
        high = lax.ppermute(lax.slice_in_dim(block, 0, width, axis=dim), axis, backward)
        block = jnp.concatenate([low, block, high], axis=dim)
    return block


def cut_along(value, dim, size):
    before, after = (value.shape[:dim], value.shape[dim + 1 :])
    return jnp.moveaxis(value.reshape(*before, size, -1, *after), dim, 0)


def sent_and_summed(value, axis, dim):
    size = lax.axis_size(axis)
    tiles = lax.all_to_all(cut_along(value, dim, size), axis, 0, 0, tiled=True)
    return jnp.sum(tiles, axis=0)


def shifted(block, axis, distance):
    devices = range(lax.axis_size(axis))
    route = [((i - distance) % len(devices), i) for i in devices]
    return lax.ppermute(block, axis, route)


def local(increment, jacobian, lat_weight, centre, west, east, lat_offset, lev_offset):
    width = increment.shape[0]
    span = 3 * width
    slots = centre.shape[0]
    band = lax.axis_index("lat")
    band_count = lax.axis_size("lat")
    rows_band = increment.shape[1]
    packed = jnp.concatenate(
        [
            lat_weight,
            lat_offset[:, None].astype(jnp.float32),
            lev_offset[:, None].astype(jnp.float32),
        ],
        axis=1,
    )
    packed_all = lax.all_gather(packed, "lat", axis=0, tiled=True)
    nearby = padded(packed_all[None], (("lon", 0),), 1)
    listed = nearby.reshape(3 * band_count * slots, BLAT + 2)
    weights = listed[:, :BLAT]
    lat_first = listed[:, BLAT].astype(jnp.int32)
    lev_first = listed[:, BLAT + 1].astype(jnp.int32)
    local_rows = lat_first[:, None] + jnp.arange(BLAT, dtype=jnp.int32)[None, :] - band * rows_band
    selector = (
        local_rows[:, :, None] == jnp.arange(rows_band, dtype=jnp.int32)[None, None, :]
    ).astype(jnp.float32)
    row_weight = jnp.einsum("nj,nji->ni", weights, selector, precision=lax.Precision.HIGHEST)
    lifted = jnp.einsum(
        "ni,cik->nck", row_weight, increment.astype(jnp.float32), precision=lax.Precision.HIGHEST
    )

    def level_box(column_block, first):
        return lax.dynamic_slice_in_dim(column_block, first, BLEV, 1)

    partial_value = jax.vmap(level_box)(lifted, lev_first).reshape(
        3, band_count, slots, width, BLEV
    )
    summed = sent_and_summed(partial_value, "lat", 1)[:, 0]
    pieces = summed.astype(jnp.bfloat16)
    from_east = shifted(pieces[0], "lon", -1)
    from_west = shifted(pieces[2], "lon", 1)
    profile = jnp.concatenate([from_west, pieces[1], from_east], axis=1)
    rows = jnp.arange(span, dtype=jnp.int32)[None, :]
    keep = (rows >= width + centre[:, None] - west[:, None]) & (
        rows <= width + centre[:, None] + east[:, None]
    )
    profile = jnp.where(keep[:, :, None], profile, jnp.zeros_like(profile))
    flat_profile = profile.reshape(slots, span * BLEV)
    return jnp.einsum("str,sr->st", jacobian, flat_profile, preferred_element_type=jnp.float32)


def solution(mesh):
    return jax.shard_map(
        local,
        mesh=mesh,
        in_specs=(
            P("lon", "lat", None),
            P(("lon", "lat"), None, None),
            P(("lon", "lat"), None),
            P(("lon", "lat")),
            P(("lon", "lat")),
            P(("lon", "lat")),
            P(("lon", "lat")),
            P(("lon", "lat")),
        ),
        out_specs=P(("lon", "lat"), None),
        check_vma=False,
    )
```

profile of v0, /device:TPU:8, one launch (start us, length us, event | category | flops | bytes accessed | tf_op | source)
XLA Modules:
  0.0 106.0 jit_solution(16492444207678845187)
XLA Ops:
  0.0 0.7 convert_bitcast_fusion.1
  0.7 0.7 convert_bitcast_fusion
  1.6 0.8 copy.23
  2.4 5.4 %all_gather.3 = f32[64,10]{1,0:T(8,128)S(1)} all-gather(f32[16,10]{1,0:T(8,128)S(1)} %pad_maximum_fusion.1), channel_id=1, replica_groups=mesh['lon'=64,'lat'=4] {'lat'}, dimensions={0}, use_global_device_ids=true | all-gather | bytes 3200 | tf_op jit(solution)/shard_map/all_gather | solution.py:56
  7.8 9.6 %collective-permute-start.1 = (f32[1,64,10]{2,1,0:T(8,128)S(1)}, f32[1,64,10]{2,1,0:T(8,128)S(1)}, u32[]{:S(2)}, u32[]{:S(2)}) collective-permute-start(f32[1,64,10]{2,1,0:T(8,128)S(1)} %bitcast.41), channel_id=1, source_target_pairs={{4,0},{8,4},{12,8},{16,12},{20,16},{24,20},{28,24},{32,28},{36,32}... | collective-permute-start | bytes 7688 | tf_op jit(solution)/shard_map/ppermute | solution.py:19
  17.4 1.5 %collective-permute-done.1 = f32[1,64,10]{2,1,0:T(8,128)S(1)} collective-permute-done((f32[1,64,10]{2,1,0:T(8,128)S(1)}, f32[1,64,10]{2,1,0:T(8,128)S(1)}, u32[]{:S(2)}, u32[]{:S(2)}) %collective-permute-start.1) | collective-permute-done | bytes 2592 | tf_op jit(solution)/shard_map/ppermute | solution.py:19
  19.0 8.0 %collective-permute-done = f32[1,64,10]{2,1,0:T(8,128)S(1)} collective-permute-done((f32[1,64,10]{2,1,0:T(8,128)S(1)}, f32[1,64,10]{2,1,0:T(8,128)S(1)}, u32[]{:S(2)}, u32[]{:S(2)}) %collective-permute-start) | collective-permute-done | bytes 2592 | tf_op jit(solution)/shard_map/ppermute | solution.py:16
  27.4 0.8 fusion
  28.3 3.0 %fusion.7 = f32[192,32,128]{2,0,1:T(8,128)} fusion(f32[192,128,1]{1,0,2:T(8,128)S(1)} %bitcast.44, bf16[32,128,128]{2,1,0:T(8,128)(2,1)S(1)} %copy-done), kind=kOutput, calls=%fused_computation.28 | convolution fusion | flops 1207959552 | bytes 4292608 | tf_op jit(solution)/shard_map/ni,cik->nck/dot_general | solution.py:67
  31.3 11.5 %copy.29 = f32[192,32,128]{1,0,2:T(8,128)} copy(f32[192,32,128]{2,0,1:T(8,128)} %fusion.7) | data formatting | bytes 6291456 | tf_op jit(solution)/shard_map/ni,cik->nck/dot_general | solution.py:67
  42.9 13.2 %gather_fusion = f32[192,32,32]{1,0,2:T(8,128)} fusion(f32[192,32,128]{1,0,2:T(8,128)} %copy.29, s32[192]{0:T(256)S(1)} %bitcast.40), kind=kCustom, calls=%fused_computation | custom fusion | bytes 1575168 | tf_op jit(solution)/shard_map/vmap()/gather | solution.py:72
  56.0 3.8 %copy.44 = f32[3,4,1,16,32,32]{4,3,0,5,2,1:T(8,128)} copy(f32[3,4,1,16,32,32]{4,3,1,0,5,2:T(8,128)} %bitcast.39) | data formatting | bytes 1572864 | tf_op jit(solution)/shard_map/reshape;reshape | solution.py:26
  59.9 4.4 %reshape.95 = f32[4,1,49152]{2,1,0:T(1,128)} reshape(f32[4,1,32,3,16,32]{5,4,3,2,1,0:T(8,128)} %bitcast.38) | data formatting | bytes 1572864
  64.3 4.8 %all-to-all-start = ((f32[4,1,49152]{2,1,0:T(1,128)}), f32[4,1,49152]{2,1,0:T(1,128)S(1)}, u32[]{:S(2)}, u32[]{:S(2)}) async-start(f32[4,1,49152]{2,1,0:T(1,128)} %reshape.95), calls=%async_computation | async-start | bytes 1572864 | tf_op jit(solution)/shard_map/all_to_all | solution.py:31
  69.1 10.0 %all-to-all-done = f32[4,1,49152]{2,1,0:T(1,128)S(1)} async-done(((f32[4,1,49152]{2,1,0:T(1,128)}), f32[4,1,49152]{2,1,0:T(1,128)S(1)}, u32[]{:S(2)}, u32[]{:S(2)}) %all-to-all-start) | async-done | bytes 786464 | tf_op jit(solution)/shard_map/all_to_all | solution.py:31
  79.1 0.5 broadcast.92
  79.6 2.9 %reduce.1 = f32[4,49152]{1,0:T(4,128)S(1)} reduce(f32[4,1,49152]{2,1,0:T(1,128)S(1)} %all-to-all-done, f32[]{:T(128)} %broadcast.92), dimensions={1}, to_apply=%all_to_all.3.reduce_sub_computation | reduce | bytes 1572868 | tf_op jit(solution)/shard_map/all_to_all | solution.py:31
  82.5 2.7 %reshape.96 = f32[4,1,32,3,16,32]{5,4,3,2,1,0:T(8,128)} reshape(f32[4,49152]{1,0:T(4,128)S(1)} %reduce.1) | data formatting | bytes 1572864
  85.3 2.1 %bitcast_reduce_fusion = bf16[3,16,32,32]{2,1,0,3:T(8,128)(2,1)S(1)} fusion(f32[4,1,32,3,16,32]{5,4,3,2,1,0:T(8,128)} %reshape.96), kind=kLoop, calls=%fused_computation.26 | loop fusion | flops 147456 | bytes 884736 | tf_op jit(solution)/shard_map/reduce_sum | solution.py:32
  87.5 7.7 %collective-permute-start.3 = (bf16[16,32,32]{1,0,2:T(8,128)(2,1)S(1)}, bf16[16,32,32]{1,0,2:T(8,128)(2,1)S(1)}, u32[]{:S(2)}, u32[]{:S(2)}) collective-permute-start(bf16[16,32,32]{1,0,2:T(8,128)(2,1)S(1)} %get-tuple-element.7), channel_id=1, source_target_pairs={{4,0},{8,4},{12,8},{16,12},{20,16},{24,20},{28,24},{32,28},{36,32}... | collective-permute-start | bytes 98312 | tf_op jit(solution)/shard_map/ppermute | solution.py:38
  95.4 3.0 %collective-permute-done.2 = bf16[16,32,32]{1,0,2:T(8,128)(2,1)S(1)} collective-permute-done((bf16[16,32,32]{1,0,2:T(8,128)(2,1)S(1)}, bf16[16,32,32]{1,0,2:T(8,128)(2,1)S(1)}, u32[]{:S(2)}, u32[]{:S(2)}) %collective-permute-start.2) | collective-permute-done | bytes 32800 | tf_op jit(solution)/shard_map/ppermute | solution.py:38
  98.6 0.2 copy.35
  98.8 0.2 reshape.94
  99.1 7.0 %fusion.8 = f32[16,1,128]{2,1,0:T(1,128)} fusion(bf16[16,3072,1]{1,2,0:T(2,128)(2,1)S(1)} %reshape.94, bf16[16,128,3072]{2,1,0:T(8,128)(2,1)} %param.9), kind=kOutput, calls=%fused_computation.29 | convolution fusion | flops 12582912 | bytes 12689408 | tf_op jit(solution)/shard_map/str,sr->st/dot_general | solution.py:88
  (31 shorter events, 1.3 us)
Async XLA Ops:
  0.0 28.3 %copy-start = (bf16[32,128,128]{2,1,0:T(8,128)(2,1)S(1)}, bf16[32,128,128]{2,1,0:T(8,128)(2,1)}, u32[]{:S(2)}) copy-start(bf16[32,128,128]{2,1,0:T(8,128)(2,1)} %param.8) | copy-start | bytes 3145732
  7.8 11.2 %collective-permute-start.1 = (f32[1,64,10]{2,1,0:T(8,128)S(1)}, f32[1,64,10]{2,1,0:T(8,128)S(1)}, u32[]{:S(2)}, u32[]{:S(2)}) collective-permute-start(f32[1,64,10]{2,1,0:T(8,128)S(1)} %bitcast.41), channel_id=1, source_target_pairs={{4,0},{8,4},{12,8},{16,12},{20,16},{24,20},{28,24},{32,28},{36,32}... | collective-permute-start | bytes 7688 | tf_op jit(solution)/shard_map/ppermute | solution.py:19
  17.4 9.6 %collective-permute-start = (f32[1,64,10]{2,1,0:T(8,128)S(1)}, f32[1,64,10]{2,1,0:T(8,128)S(1)}, u32[]{:S(2)}, u32[]{:S(2)}) collective-permute-start(f32[1,64,10]{2,1,0:T(8,128)S(1)} %bitcast.42), channel_id=1, source_target_pairs={{0,4},{4,8},{8,12},{12,16},{16,20},{20,24},{24,28},{28,32},{32,36}... | collective-permute-start | bytes 7688 | tf_op jit(solution)/shard_map/ppermute | solution.py:16
  59.9 9.2 %copy-start.1 = (s32[16]{0:T(128)S(1)}, s32[16]{0:T(128)}, u32[]{:S(2)}) copy-start(s32[16]{0:T(128)} %param.12) | copy-start | bytes 196
  59.9 9.2 %copy-start.2 = (s32[16]{0:T(128)S(1)}, s32[16]{0:T(128)}, u32[]{:S(2)}) copy-start(s32[16]{0:T(128)} %param.11) | copy-start | bytes 196
  59.9 9.2 %copy-start.3 = (s32[16]{0:T(128)S(1)}, s32[16]{0:T(128)}, u32[]{:S(2)}) copy-start(s32[16]{0:T(128)} %param.13) | copy-start | bytes 196
  64.3 14.8 %all-to-all-start = ((f32[4,1,49152]{2,1,0:T(1,128)}), f32[4,1,49152]{2,1,0:T(1,128)S(1)}, u32[]{:S(2)}, u32[]{:S(2)}) async-start(f32[4,1,49152]{2,1,0:T(1,128)} %reshape.95), calls=%async_computation | async-start | bytes 1572864 | tf_op jit(solution)/shard_map/all_to_all | solution.py:31
  87.4 10.9 %collective-permute-start.2 = (bf16[16,32,32]{1,0,2:T(8,128)(2,1)S(1)}, bf16[16,32,32]{1,0,2:T(8,128)(2,1)S(1)}, u32[]{:S(2)}, u32[]{:S(2)}) collective-permute-start(bf16[16,32,32]{1,0,2:T(8,128)(2,1)S(1)} %get-tuple-element.5), channel_id=1, source_target_pairs={{252,0},{0,4},{4,8},{8,12},{12,16},{16,20},{20,24},{24,28},{28,32}... | collective-permute-start | bytes 98312 | tf_op jit(solution)/shard_map/ppermute | solution.py:38
  87.5 10.9 %collective-permute-start.3 = (bf16[16,32,32]{1,0,2:T(8,128)(2,1)S(1)}, bf16[16,32,32]{1,0,2:T(8,128)(2,1)S(1)}, u32[]{:S(2)}, u32[]{:S(2)}) collective-permute-start(bf16[16,32,32]{1,0,2:T(8,128)(2,1)S(1)} %get-tuple-element.7), channel_id=1, source_target_pairs={{4,0},{8,4},{12,8},{16,12},{20,16},{24,20},{28,24},{32,28},{36,32}... | collective-permute-start | bytes 98312 | tf_op jit(solution)/shard_map/ppermute | solution.py:38
where the time goes:
time: 107 us; the launch traced here: 106 us
  local copies, waits for them, and re-layouts  38.1 us (36%)
  waiting for transfers between devices  22.4 us (21%)
  starting transfers between devices  22.2 us (21%)
  matrix products  10.8 us (10%)
  other arithmetic  6.88 us (6%)
  blocking collectives  5.38 us (5%)
    gather x1, local copies, waits for them, and re-layouts, level_box(): return lax.dynamic_slice_in_dim(column_block, first, BLEV, 1)  13.2 us
    dot_general x1, local copies, waits for them, and re-layouts, local(): jnp.einsum('ni,cik->nck', row_weight, increment.astype(jnp.float32), prec...  11.5 us
    all_to_all x1, waiting for transfers between devices, sent_and_summed(): tiles = lax.all_to_all(cut_along(value, dim, size), axis, 0, 0, tiled=True)  9.97 us
    ppermute x1, starting transfers between devices, padded(): lax.ppermute(lax.slice_in_dim(block, 0, width, axis=dim), axis, backward)  9.58 us
    ppermute x1, waiting for transfers between devices, padded(): lax.ppermute(lax.slice_in_dim(block, block.shape[dim] - width, None, axis...  7.97 us
    unnamed x11, local copies, waits for them, and re-layouts  7.91 us
    ppermute x2, starting transfers between devices, shifted(): return lax.ppermute(block, axis, route)  7.82 us
    dot_general x1, matrix products, local(): jnp.einsum('str,sr->st', jacobian, flat_profile, preferred_element_type=j...  6.95 us
  transfers between devices with their start and end apart: 5, of which 4 were waited for; matrix products, arithmetic and copies ran while one was open for 0% of the time, Pallas kernels for 0%

commit v1 on v0

v1 whole, which is shorter than its diff:
```python
import functools

import jax
import jax.numpy as jnp
from jax import lax
from jax.experimental import pallas as pl
from jax.experimental.pallas import tpu as pltpu
from jax.sharding import PartitionSpec as P

BLAT = 8
BLEV = 32
AXES = ("lon", "lat")


def select_kernel(count, band_ref, meta_ref, own_ref, pair_ref, mine_ref, other_ref):
    width, rows, _ = own_ref.shape
    half = mine_ref.shape[0]
    meta = jnp.transpose(meta_ref[...])[:count]
    band = band_ref[0]
    lat_first = meta[:, BLAT : BLAT + 1].astype(jnp.int32)
    lev_first = meta[:, BLAT + 1 : BLAT + 2].astype(jnp.int32)
    lane = lax.broadcasted_iota(jnp.int32, (count, 128), 1)

    def weights(first):
        offset = lane + first - lat_first
        total = jnp.zeros((count, 128), jnp.float32)
        for j in range(BLAT):
            total = jnp.where(offset == j, meta[:, j : j + 1], total)
        return total

    full = jnp.concatenate(
        [weights(band * rows), weights((band + 1 - 2 * lax.rem(band, 2)) * rows)], axis=1
    )
    high = full.astype(jnp.bfloat16)
    low = (full - high.astype(jnp.float32)).astype(jnp.bfloat16)
    left = jnp.concatenate([high, low], axis=0)
    index = lev_first + lax.rem(lane, BLEV)
    spot = lane // BLEV
    for q in range(width // 4):
        tile = None
        for h in range(2):
            c = 4 * q + 2 * h
            right = jnp.concatenate(
                [
                    jnp.concatenate([own_ref[c], pair_ref[c]], axis=0),
                    jnp.concatenate([own_ref[c + 1], pair_ref[c + 1]], axis=0),
                ],
                axis=1,
            )
            both = jnp.dot(left, right, preferred_element_type=jnp.float32)
            both = both[:count] + both[count:]
            for i in range(2):
                box = jnp.take_along_axis(both[:, 128 * i : 128 * i + 128], index, axis=1)
                tile = box if tile is None else jnp.where(spot == 2 * h + i, box, tile)
        tile_at = slice(128 * q, 128 * q + 128)
        for g in range(half // 16):
            mine_ref[16 * g : 16 * g + 16, tile_at] = tile[32 * g : 32 * g + 16]
            other_ref[16 * g : 16 * g + 16, tile_at] = tile[32 * g + 16 : 32 * g + 32]


def select(band, meta, own, pair, count):
    meta = jnp.pad(meta, ((0, 16 - meta.shape[0]), (0, 128 - meta.shape[1])))
    width = own.shape[0]
    out = jax.ShapeDtypeStruct((count // 2, width * BLEV), jnp.float32)
    vmem = pl.BlockSpec(memory_space=pltpu.VMEM)
    return pl.pallas_call(
        functools.partial(select_kernel, count),
        out_shape=(out, out),
        in_specs=[pl.BlockSpec(memory_space=pltpu.SMEM), vmem, vmem, vmem],
        out_specs=(vmem, vmem),
        compiler_params=pltpu.CompilerParams(vmem_limit_bytes=12 * 1024 * 1024),
        cost_estimate=pl.CostEstimate(
            flops=2 * count * 256 * 128 * width * 2, bytes_accessed=2 * 1024 * 1024, transcendentals=0
        ),
        name="select",
    )(band, meta, own, pair)


def contract_kernel(parts, info_ref, jac_ref, *refs):
    pieces, out_ref, prof_ref = refs[:parts], refs[parts], refs[parts + 1]
    slots, tangents, lanes = out_ref.shape[0], out_ref.shape[1], 128
    odd = info_ref[3, 0]
    for piece, place in zip(pieces, (lax.mul(odd, 2), 1, lax.mul(1 - odd, 2))):
        start = pl.multiple_of(place * 1024, 1024)
        prof_ref[:, pl.ds(start, 1024)] = piece[...].astype(jnp.float32)
    column = lax.broadcasted_iota(jnp.int32, (1, lanes), 1) // BLEV
    place = lax.broadcasted_iota(jnp.int32, (tangents, lanes), 1)
    result = jnp.zeros((tangents, lanes), jnp.float32)
    for s in range(slots):
        first = 32 + info_ref[0, s] - info_ref[1, s]
        last = 32 + info_ref[0, s] + info_ref[2, s]

        def step(t, total):
            at = pl.multiple_of(t * lanes, lanes)
            row = prof_ref[s : s + 1, pl.ds(at, lanes)]
            r = column + 4 * t
            row = jnp.where((r >= first) & (r <= last), row, 0.0)
            return total + jac_ref[s, :, pl.ds(at, lanes)].astype(jnp.float32) * row

        total = lax.fori_loop(
            first // 4, last // 4 + 1, step, jnp.zeros((tangents, lanes), jnp.float32)
        )
        result = jnp.where(place == s, jnp.sum(total, axis=1, keepdims=True), result)
    out_ref[...] = jnp.transpose(result)[:slots]


def contract(info, jacobian, far, own, near):
    slots, tangents, depth = jacobian.shape
    vmem = pl.BlockSpec(memory_space=pltpu.VMEM)
    return pl.pallas_call(
        functools.partial(contract_kernel, 3),
        out_shape=jax.ShapeDtypeStruct((slots, tangents), jnp.float32),
        in_specs=[pl.BlockSpec(memory_space=pltpu.SMEM)] + [vmem] * 4,
        out_specs=vmem,
        scratch_shapes=[pltpu.VMEM((slots, depth), jnp.float32)],
        compiler_params=pltpu.CompilerParams(vmem_limit_bytes=20 * 1024 * 1024),
        cost_estimate=pl.CostEstimate(flops=2 * slots * tangents * depth, bytes_accessed=12582912, transcendentals=0),
        name="contract",
    )(info, jacobian, far, own, near)


def local(increment, jacobian, lat_weight, centre, west, east, lat_offset, lev_offset):
    n_lon, n_lat = lax.axis_size("lon"), lax.axis_size("lat")
    band = lax.axis_index("lat")
    odd = lax.rem(lax.axis_index("lon"), 2)

    def within(flip):
        return [(a * n_lat + b, a * n_lat + (b ^ flip)) for a in range(n_lon) for b in range(n_lat)]

    def swaps(start):
        pairs = [(a % n_lon, (a + 1) % n_lon) for a in range(start, n_lon, 2)]
        return pairs + [(b, a) for a, b in pairs]

    def across(value):
        return lax.ppermute(value, AXES, within(2))

    meta = jnp.concatenate(
        [
            lat_weight.T,
            lat_offset[None].astype(jnp.float32),
            lev_offset[None].astype(jnp.float32),
        ],
        axis=0,
    )
    meta = jnp.concatenate([meta, across(meta)], axis=1)
    pair = lax.ppermute(increment, AXES, within(1))
    meta_far = lax.ppermute(meta, "lon", swaps(1))
    meta_near = lax.ppermute(meta, "lon", swaps(0))
    bands = band[None].astype(jnp.int32)

    mine, other = select(bands, jnp.concatenate([meta, meta_near], axis=1), increment, pair, 64)
    near = (mine + across(other)).astype(jnp.bfloat16)
    own, near = near[:16], lax.ppermute(near[16:], "lon", swaps(0))
    mine, other = select(bands, meta_far, increment, pair, 32)
    far = lax.ppermute((mine + across(other)).astype(jnp.bfloat16), "lon", swaps(1))

    info = jnp.stack([centre, west, east, jnp.broadcast_to(odd, centre.shape).astype(jnp.int32)])
    return contract(info, jacobian, far, own, near)


def solution(mesh):
    return jax.shard_map(
        local,
        mesh=mesh,
        in_specs=(
            P("lon", "lat", None),
            P(("lon", "lat"), None, None),
            P(("lon", "lat"), None),
            P(("lon", "lat")),
            P(("lon", "lat")),
            P(("lon", "lat")),
            P(("lon", "lat")),
            P(("lon", "lat")),
        ),
        out_specs=P(("lon", "lat"), None),
        check_vma=False,
    )
```

time: 107 us -> 45.8 us (0.43)
  local copies, waits for them, and re-layouts: 38.1 us -> 7.11 us
  waiting for transfers between devices: 22.4 us -> 6.33 us
  matrix products: 10.8 us -> 0 us
  Pallas kernels: 0 us -> 6.49 us
  blocking collectives: 5.38 us -> 0 us
  other arithmetic: 6.88 us -> 3.68 us
    gather x1 -> x0, local copies, waits for them, and re-layouts: 13.2 us -> none  [level_box(): return lax.dynamic_slice_in_dim(column_block, first, BLEV, 1)]
    dot_general x1 -> x0, local copies, waits for them, and re-layouts: 11.5 us -> none  [local(): jnp.einsum('ni,cik->nck', row_weight, increment.astype(jnp.float32), prec...]
    dot_general x3 -> x0, matrix products: 10.8 us -> none  [the longest x1 6.95 us: local(): jnp.einsum('str,sr->st', jacobian, flat_profile, preferred_element_type=j...]
    all_to_all x1 -> x0, waiting for transfers between devices: 9.97 us -> none  [sent_and_summed(): tiles = lax.all_to_all(cut_along(value, dim, size), axis, 0, 0, tiled=True)]
    pallas_call x0 -> x3, Pallas kernels: none -> 6.49 us  [the longest x1 4.8 us: contract(): pl.pallas_call(functools.partial(contract_kernel, 3), out_shape=jax.Shape...]
    ppermute x4 -> x8, waiting for transfers between devices: 12.5 us -> 6.33 us  [the longest x1 2.14 us: local(): own, near = (near[:16], lax.ppermute(near[16:], 'lon', swaps(0)))]
    all_gather x1 -> x0, blocking collectives: 5.38 us -> none  [local(): packed_all = lax.all_gather(packed, 'lat', axis=0, tiled=True)]
    all_to_all x1 -> x0, starting transfers between devices: 4.81 us -> none  [sent_and_summed(): tiles = lax.all_to_all(cut_along(value, dim, size), axis, 0, 0, tiled=True)]
  transfers between devices with their start and end apart: 5 -> 8, of which waited for: 4 -> 4; matrix products, arithmetic and copies ran while one was open for 0% -> 8% of each run, Pallas kernels for 0% -> 4%
where the time goes in v1:
time: 45.8 us; the launch traced here: 45.6 us
  starting transfers between devices  22 us (48%)
  local copies, waits for them, and re-layouts  7.11 us (16%)
  Pallas kernels  6.49 us (14%)
  waiting for transfers between devices  6.33 us (14%)
  other arithmetic  3.68 us (8%)
    ppermute x1, starting transfers between devices, local(): meta_far = lax.ppermute(meta, 'lon', swaps(1))  9.67 us
    ppermute x1, starting transfers between devices, local(): lax.ppermute((mine + across(other)).astype(jnp.bfloat16), 'lon', swaps(1))  7.82 us
    unnamed x6, local copies, waits for them, and re-layouts  7.02 us
    pallas_call x1, Pallas kernels, contract(): pl.pallas_call(functools.partial(contract_kernel, 3), out_shape=jax.Shape...  4.8 us
    ppermute x3, starting transfers between devices, across(): return lax.ppermute(value, AXES, within(2))  4.36 us
    ppermute x1, waiting for transfers between devices, local(): own, near = (near[:16], lax.ppermute(near[16:], 'lon', swaps(0)))  2.14 us
    pallas_call x2, Pallas kernels, select(): pl.pallas_call(functools.partial(select_kernel, count), out_shape=(out, o...  1.68 us
    ppermute x3, waiting for transfers between devices, across(): return lax.ppermute(value, AXES, within(2))  1.63 us
  transfers between devices with their start and end apart: 8, of which 4 were waited for; matrix products, arithmetic and copies ran while one was open for 8% of the time, Pallas kernels for 4%

profile of v1, /device:TPU:8, one launch (start us, length us, event | category | flops | bytes accessed | tf_op | source)
XLA Modules:
  0.0 45.6 jit_solution(5145743136688866132)
XLA Ops:
  0.0 0.0 collective-permute-start.2
  0.0 0.7 %convert_bitcast_fusion = (f32[1,16]{1,0:T(1,128)S(1)}, f32[1,16]{1,0:T(1,128)S(1)}) fusion(s32[16]{0:T(128)} %param.15, s32[16]{0:T(128)} %param.14), kind=kLoop, calls=%fused_computation.11 | loop fusion | flops 32 | bytes 256 | tf_op jit(solution)/shard_map/convert_element_type | solution.py:141
  0.7 0.7 %pad_maximum_fusion = f32[10,16]{1,0:T(8,128)S(1)} fusion(f32[1,16]{1,0:T(1,128)S(1)} %get-tuple-element.15, f32[1,16]{1,0:T(1,128)S(1)} %get-tuple-element.16, f32[8,16]{1,0:T(8,128)} %bitcast.10), kind=kLoop, calls=%fused_computation.8 | loop fusion | flops 320 | bytes 1280 | tf_op jit(solution)/shard_map/concatenate | solution.py:137
  1.4 2.2 %collective-permute-start = (f32[10,16]{1,0:T(8,128)S(1)}, f32[10,16]{1,0:T(8,128)S(1)}, u32[]{:S(2)}, u32[]{:S(2)}) collective-permute-start(f32[10,16]{1,0:T(8,128)S(1)} %pad_maximum_fusion), channel_id=1, source_target_pairs={{0,2},{1,3},{2,0},{3,1},{4,6},{5,7},{6,4},{7,5},{8,10},{9,11},{10,... | collective-permute-start | bytes 1928 | tf_op jit(solution)/shard_map/ppermute | solution.py:135
  3.5 1.6 %collective-permute-done = f32[10,16]{1,0:T(8,128)S(1)} collective-permute-done((f32[10,16]{1,0:T(8,128)S(1)}, f32[10,16]{1,0:T(8,128)S(1)}, u32[]{:S(2)}, u32[]{:S(2)}) %collective-permute-start) | collective-permute-done | bytes 672 | tf_op jit(solution)/shard_map/ppermute | solution.py:135
  5.2 0.8 %pad_maximum_fusion.1 = f32[10,32]{1,0:T(8,128)S(1)} fusion(f32[10,16]{1,0:T(8,128)S(1)} %collective-permute-done, f32[1,16]{1,0:T(1,128)S(1)} %get-tuple-element.15, f32[1,16]{1,0:T(1,128)S(1)} %get-tuple-element.16, f32[8,16]{1,0:T(8,128)} %bitcast.11), kind=kLoop, calls=%fused_computation.9 | loop fusion | flops 960 | bytes 2560 | tf_op jit(solution)/shard_map/concatenate | solution.py:145
  5.9 9.7 %collective-permute-start.1 = (f32[10,32]{1,0:T(8,128)S(1)}, f32[10,32]{1,0:T(8,128)S(1)}, u32[]{:S(2)}, u32[]{:S(2)}) collective-permute-start(f32[10,32]{1,0:T(8,128)S(1)} %pad_maximum_fusion.1), channel_id=1, source_target_pairs={{4,8},{12,16},{20,24},{28,32},{36,40},{44,48},{52,56},{60,64},{68,... | collective-permute-start | bytes 3848 | tf_op jit(solution)/shard_map/ppermute | solution.py:147
  15.6 0.1 pad.25.clone
  15.7 1.6 %collective-permute-done.1 = f32[10,32]{1,0:T(8,128)S(1)} collective-permute-done((f32[10,32]{1,0:T(8,128)S(1)}, f32[10,32]{1,0:T(8,128)S(1)}, u32[]{:S(2)}, u32[]{:S(2)}) %collective-permute-start.1) | collective-permute-done | bytes 1312 | tf_op jit(solution)/shard_map/ppermute | solution.py:147
  17.2 0.0 copy-start.1
  17.2 1.2 %copy-done.1 = bf16[32,128,128]{2,1,0:T(8,128)(2,1)S(1)} copy-done((bf16[32,128,128]{2,1,0:T(8,128)(2,1)S(1)}, bf16[32,128,128]{2,1,0:T(8,128)(2,1)}, u32[]{:S(2)}) %copy-start.1) | copy-done | bytes 1048600
  18.5 0.7 %select.32 = (f32[16,1024]{1,0:T(8,128)S(1)}, f32[16,1024]{1,0:T(8,128)S(1)}) custom-call(s32[1]{0:T(128)} %bitcast.3.band_ref, f32[16,128]{1,0:T(8,128)S(1)} %pad.8.meta_ref, bf16[32,128,128]{2,1,0:T(8,128)(2,1)S(1)} %copy-done.1, bf16[32,128,128]{2,1,0:T(8,128)(2,1)S(1)} %collective-permute-done.2.pair_ref), custom_call_target="tpu_custom_call" | custom-call | flops 134217728 | bytes 2097152 | tf_op jit(solution)/shard_map/select/pallas_call | solution.py:66
  19.2 1.4 %collective-permute-start.3 = (f32[16,1024]{1,0:T(8,128)S(1)}, f32[16,1024]{1,0:T(8,128)S(1)}, u32[]{:S(2)}, u32[]{:S(2)}) collective-permute-start(f32[16,1024]{1,0:T(8,128)S(1)} %get-tuple-element.10), channel_id=1, source_target_pairs={{0,2},{1,3},{2,0},{3,1},{4,6},{5,7},{6,4},{7,5},{8,10},{9,11},{10,... | collective-permute-start | bytes 196616 | tf_op jit(solution)/shard_map/ppermute | solution.py:135
  20.6 0.8 %select_maximum_fusion.meta_ref = f32[16,128]{1,0:T(8,128)S(1)} fusion(f32[10,32]{1,0:T(8,128)S(1)} %collective-permute-done.5, f32[10,16]{1,0:T(8,128)S(1)} %collective-permute-done, f32[1,16]{1,0:T(1,128)S(1)} %get-tuple-element.15, f32[1,16]{1,0:T(1,128)S(1)} %get-tuple-element.16, f32[8,16]{1,0:T(8,128)} %bitcast.12), kind=kLoop, calls=%fused_computation.2 | loop fusion | flops 34816 | bytes 10752 | tf_op jit(solution)/shard_map/concatenate | solution.py:151
  21.4 1.2 %copy-done.2 = bf16[32,128,128]{2,1,0:T(8,128)(2,1)S(1)} copy-done((bf16[32,128,128]{2,1,0:T(8,128)(2,1)S(1)}, bf16[32,128,128]{2,1,0:T(8,128)(2,1)}, u32[]{:S(2)}) %copy-start.2) | copy-done | bytes 1048600
  22.6 1.0 %select.33 = (f32[32,1024]{1,0:T(8,128)S(1)}, f32[32,1024]{1,0:T(8,128)S(1)}) custom-call(s32[1]{0:T(128)} %bitcast.3.band_ref, f32[16,128]{1,0:T(8,128)S(1)} %select_maximum_fusion.meta_ref, bf16[32,128,128]{2,1,0:T(8,128)(2,1)S(1)} %copy-done.2, bf16[32,128,128]{2,1,0:T(8,128)(2,1)S(1)} %collective-permute-done.2.pair_ref), custom_call_target="tpu_custom_call" | custom-call | flops 268435456 | bytes 2097152 | tf_op jit(solution)/shard_map/select/pallas_call | solution.py:66
  23.6 0.8 %collective-permute-start.6 = (f32[32,1024]{1,0:T(8,128)S(1)}, f32[32,1024]{1,0:T(8,128)S(1)}, u32[]{:S(2)}, u32[]{:S(2)}) collective-permute-start(f32[32,1024]{1,0:T(8,128)S(1)} %get-tuple-element.12), channel_id=1, source_target_pairs={{0,2},{1,3},{2,0},{3,1},{4,6},{5,7},{6,4},{7,5},{8,10},{9,11},{10,... | collective-permute-start | bytes 393224 | tf_op jit(solution)/shard_map/ppermute | solution.py:135
  24.4 7.8 %collective-permute-start.4 = (bf16[16,1024]{1,0:T(8,128)(2,1)S(1)}, bf16[16,1024]{1,0:T(8,128)(2,1)S(1)}, u32[]{:S(2)}, u32[]{:S(2)}) collective-permute-start(bf16[16,1024]{1,0:T(8,128)(2,1)S(1)} %add_convert_fusion.1), channel_id=1, source_target_pairs={{4,8},{12,16},{20,24},{28,32},{36,40},{44,48},{52,56},{60,64},{68,... | collective-permute-start | bytes 98312 | tf_op jit(solution)/shard_map/ppermute | solution.py:155
  32.2 0.1 collective-permute-start.7
  32.3 0.8 %add_add_fusion.info_ref = s32[4,16]{1,0:T(4,128)S(1)} fusion(s32[1,16]{1,0:T(1,128)} %bitcast.13, s32[1,16]{1,0:T(1,128)} %bitcast.14, s32[1,16]{1,0:T(1,128)} %bitcast.15, s32[4]{0:T(128)S(1)} %pad.25.clone), kind=kLoop, calls=%fused_computation.10 | loop fusion | flops 192 | bytes 464 | tf_op jit(solution)/shard_map/stack | solution.py:157
  33.1 1.0 %collective-permute-done.4.refs_0_ = bf16[16,1024]{1,0:T(8,128)(2,1)S(1)} collective-permute-done((bf16[16,1024]{1,0:T(8,128)(2,1)S(1)}, bf16[16,1024]{1,0:T(8,128)(2,1)S(1)}, u32[]{:S(2)}, u32[]{:S(2)}) %collective-permute-start.4) | collective-permute-done | bytes 32800 | tf_op jit(solution)/shard_map/ppermute | solution.py:155
  34.1 2.1 %collective-permute-done.7.refs_2_ = bf16[16,1024]{1,0:T(8,128)(2,1)S(1)} collective-permute-done((bf16[16,1024]{1,0:T(8,128)(2,1)S(1)}, bf16[16,1024]{1,0:T(8,128)(2,1)S(1)}, u32[]{:S(2)}, u32[]{:S(2)}) %collective-permute-start.7) | collective-permute-done | bytes 32800 | tf_op jit(solution)/shard_map/ppermute | solution.py:153
  36.2 4.6 %copy-done = bf16[16,128,3072]{2,1,0:T(8,128)(2,1)S(1)} copy-done((bf16[16,128,3072]{2,1,0:T(8,128)(2,1)S(1)}, bf16[16,128,3072]{2,1,0:T(8,128)(2,1)}, u32[]{:S(2)}) %copy-start) | copy-done | bytes 12582936
  40.8 4.8 %contract.1 = f32[16,128]{1,0:T(8,128)} custom-call(s32[4,16]{1,0:T(4,128)S(1)} %add_add_fusion.info_ref, bf16[16,128,3072]{2,1,0:T(8,128)(2,1)S(1)} %copy-done, bf16[16,1024]{1,0:T(8,128)(2,1)S(1)} %collective-permute-done.4.refs_0_, bf16[16,1024]{1,0:T(8,128)(2,1)S(1)} %get-tuple-element.14.refs_1_, bf16[16,1024]{1,0:T(8,128)(2,1)S(1)} %collective-permute-done.7.refs_2_), custom_call_target="tpu_custom_call" | custom-call | flops 12582912 | bytes 12582912 | tf_op jit(solution)/shard_map/contract/pallas_call | solution.py:110
  (11 shorter events, 0.1 us)
Async XLA Ops:
  0.0 17.2 %collective-permute-start.2 = (bf16[32,128,128]{2,1,0:T(8,128)(2,1)}, bf16[32,128,128]{2,1,0:T(8,128)(2,1)S(1)}, u32[]{:S(2)}, u32[]{:S(2)}) collective-permute-start(bf16[32,128,128]{2,1,0:T(8,128)(2,1)} %own_ref.3), channel_id=1, source_target_pairs={{0,1},{1,0},{2,3},{3,2},{4,5},{5,4},{6,7},{7,6},{8,9},{9,8},{10,11... | collective-permute-start | bytes 3145736 | tf_op jit(solution)/shard_map/ppermute | solution.py:146
  1.4 3.8 %collective-permute-start = (f32[10,16]{1,0:T(8,128)S(1)}, f32[10,16]{1,0:T(8,128)S(1)}, u32[]{:S(2)}, u32[]{:S(2)}) collective-permute-start(f32[10,16]{1,0:T(8,128)S(1)} %pad_maximum_fusion), channel_id=1, source_target_pairs={{0,2},{1,3},{2,0},{3,1},{4,6},{5,7},{6,4},{7,5},{8,10},{9,11},{10,... | collective-permute-start | bytes 1928 | tf_op jit(solution)/shard_map/ppermute | solution.py:135
  5.9 11.3 %collective-permute-start.1 = (f32[10,32]{1,0:T(8,128)S(1)}, f32[10,32]{1,0:T(8,128)S(1)}, u32[]{:S(2)}, u32[]{:S(2)}) collective-permute-start(f32[10,32]{1,0:T(8,128)S(1)} %pad_maximum_fusion.1), channel_id=1, source_target_pairs={{4,8},{12,16},{20,24},{28,32},{36,40},{44,48},{52,56},{60,64},{68,... | collective-permute-start | bytes 3848 | tf_op jit(solution)/shard_map/ppermute | solution.py:147
  15.7 5.0 %collective-permute-start.5 = (f32[10,32]{1,0:T(8,128)S(1)}, f32[10,32]{1,0:T(8,128)S(1)}, u32[]{:S(2)}, u32[]{:S(2)}) collective-permute-start(f32[10,32]{1,0:T(8,128)S(1)} %pad_maximum_fusion.1), channel_id=1, source_target_pairs={{0,4},{8,12},{16,20},{24,28},{32,36},{40,44},{48,52},{56,60},{64,6... | collective-permute-start | bytes 3848 | tf_op jit(solution)/shard_map/ppermute | solution.py:148
  17.2 1.2 %copy-start.1 = (bf16[32,128,128]{2,1,0:T(8,128)(2,1)S(1)}, bf16[32,128,128]{2,1,0:T(8,128)(2,1)}, u32[]{:S(2)}) copy-start(bf16[32,128,128]{2,1,0:T(8,128)(2,1)} %own_ref.3) | copy-start | bytes 3145732
  19.2 5.2 %collective-permute-start.3 = (f32[16,1024]{1,0:T(8,128)S(1)}, f32[16,1024]{1,0:T(8,128)S(1)}, u32[]{:S(2)}, u32[]{:S(2)}) collective-permute-start(f32[16,1024]{1,0:T(8,128)S(1)} %get-tuple-element.10), channel_id=1, source_target_pairs={{0,2},{1,3},{2,0},{3,1},{4,6},{5,7},{6,4},{7,5},{8,10},{9,11},{10,... | collective-permute-start | bytes 196616 | tf_op jit(solution)/shard_map/ppermute | solution.py:135
  21.4 1.2 %copy-start.2 = (bf16[32,128,128]{2,1,0:T(8,128)(2,1)S(1)}, bf16[32,128,128]{2,1,0:T(8,128)(2,1)}, u32[]{:S(2)}) copy-start(bf16[32,128,128]{2,1,0:T(8,128)(2,1)} %own_ref.3) | copy-start | bytes 3145732
  23.6 8.6 %collective-permute-start.6 = (f32[32,1024]{1,0:T(8,128)S(1)}, f32[32,1024]{1,0:T(8,128)S(1)}, u32[]{:S(2)}, u32[]{:S(2)}) collective-permute-start(f32[32,1024]{1,0:T(8,128)S(1)} %get-tuple-element.12), channel_id=1, source_target_pairs={{0,2},{1,3},{2,0},{3,1},{4,6},{5,7},{6,4},{7,5},{8,10},{9,11},{10,... | collective-permute-start | bytes 393224 | tf_op jit(solution)/shard_map/ppermute | solution.py:135
  24.4 9.7 %collective-permute-start.4 = (bf16[16,1024]{1,0:T(8,128)(2,1)S(1)}, bf16[16,1024]{1,0:T(8,128)(2,1)S(1)}, u32[]{:S(2)}, u32[]{:S(2)}) collective-permute-start(bf16[16,1024]{1,0:T(8,128)(2,1)S(1)} %add_convert_fusion.1), channel_id=1, source_target_pairs={{4,8},{12,16},{20,24},{28,32},{36,40},{44,48},{52,56},{60,64},{68,... | collective-permute-start | bytes 98312 | tf_op jit(solution)/shard_map/ppermute | solution.py:155
  32.2 4.0 %collective-permute-start.7 = (bf16[16,1024]{1,0:T(8,128)(2,1)S(1)}, bf16[16,1024]{1,0:T(8,128)(2,1)S(1)}, u32[]{:S(2)}, u32[]{:S(2)}) collective-permute-start(bf16[16,1024]{1,0:T(8,128)(2,1)S(1)} %get-tuple-element.13), channel_id=1, source_target_pairs={{0,4},{8,12},{16,20},{24,28},{32,36},{40,44},{48,52},{56,60},{64,6... | collective-permute-start | bytes 98312 | tf_op jit(solution)/shard_map/ppermute | solution.py:153
  36.2 4.6 %copy-start = (bf16[16,128,3072]{2,1,0:T(8,128)(2,1)S(1)}, bf16[16,128,3072]{2,1,0:T(8,128)(2,1)}, u32[]{:S(2)}) copy-start(bf16[16,128,3072]{2,1,0:T(8,128)(2,1)} %jac_ref.1) | copy-start | bytes 37748740

commit v2 on v1

v2 whole, which is shorter than its diff:
```python
import jax
import jax.numpy as jnp
from jax import lax
from jax.experimental import pallas as pl
from jax.experimental.pallas import tpu as pltpu
from jax.sharding import PartitionSpec as P


BLAT = 8
BLEV = 32
LANES = 128
COLS = LANES // BLEV
AXES = ("lon", "lat")
VMEM = pl.BlockSpec(memory_space=pltpu.VMEM)
SMEM = pl.BlockSpec(memory_space=pltpu.SMEM)


def select_kernel(meta_ref, own_ref, pair_ref, *outs):
    width, rows = own_ref.shape[0], own_ref.shape[1]
    groups = len(outs) // 2
    count = 32 * groups
    meta = jnp.transpose(meta_ref[...])[:count]
    band = lax.axis_index("lat")
    lat_first, lev_first = [meta[:, BLAT + i : BLAT + i + 1].astype(jnp.int32) for i in range(2)]
    lane = lax.broadcasted_iota(jnp.int32, (count, LANES), 1)

    def weights(first):
        offset = lane + first - lat_first
        total = jnp.zeros((count, LANES), jnp.float32)
        for j in range(BLAT):
            total = jnp.where(offset == j, meta[:, j : j + 1], total)
        return total

    full = jnp.concatenate(
        [weights(band * rows), weights((band + 1 - 2 * lax.rem(band, 2)) * rows)], axis=1
    )
    high = full.astype(jnp.bfloat16)
    low = (full - high.astype(jnp.float32)).astype(jnp.bfloat16)
    left = jnp.concatenate([high, low], axis=0)
    index = lev_first + lax.rem(lane, BLEV)
    spot = lane // BLEV
    for q in range(width // COLS):
        tile = None
        for h in range(COLS // 2):
            c = COLS * q + 2 * h
            right = jnp.concatenate(
                [
                    jnp.concatenate([own_ref[c], pair_ref[c]], axis=0),
                    jnp.concatenate([own_ref[c + 1], pair_ref[c + 1]], axis=0),
                ],
                axis=1,
            )
            both = jnp.dot(left, right, preferred_element_type=jnp.float32)
            both = both[:count] + both[count:]
            for i in range(2):
                box = jnp.take_along_axis(both[:, LANES * i : LANES * (i + 1)], index, axis=1)
                tile = box if tile is None else jnp.where(spot == 2 * h + i, box, tile)
        at = slice(LANES * q, LANES * (q + 1))
        for g in range(groups):
            outs[2 * g][:, at] = tile[32 * g : 32 * g + 16]
            outs[2 * g + 1][:, at] = tile[32 * g + 16 : 32 * g + 32]


def select(meta, own, pair):
    count = meta.shape[1]
    width = own.shape[0]
    meta = jnp.pad(meta, ((0, 0), (0, LANES - count)))
    out = jax.ShapeDtypeStruct((16, width * BLEV), jnp.float32)
    outs = count // 16
    return pl.pallas_call(
        select_kernel,
        out_shape=(out,) * outs,
        in_specs=[VMEM] * 3,
        out_specs=(VMEM,) * outs,
        compiler_params=pltpu.CompilerParams(vmem_limit_bytes=12 * 1024 * 1024),
        cost_estimate=pl.CostEstimate(
            flops=5 * 10**9, bytes_accessed=2 * 1024 * 1024, transcendentals=0
        ),
    )(meta, own, pair)


def stage_kernel(own_ref, info_ref, own_out, info_out, low_out, high_out):
    own_out[...] = own_ref[...]
    info_out[...] = info_ref[...]
    slots = low_out.shape[0]
    bounds = jnp.transpose(info_ref[...])[:slots]
    low_out[...] = jnp.broadcast_to(bounds[:, :1], low_out.shape)
    high_out[...] = jnp.broadcast_to(bounds[:, 1:2], high_out.shape)


def stage(increment, info, slots):
    bound = jax.ShapeDtypeStruct((slots, LANES), info.dtype)
    return pl.pallas_call(
        stage_kernel,
        out_shape=(
            jax.ShapeDtypeStruct(increment.shape, increment.dtype),
            jax.ShapeDtypeStruct(info.shape, info.dtype),
            bound,
            bound,
        ),
        in_specs=[VMEM, VMEM],
        out_specs=(VMEM,) * 4,
        compiler_params=pltpu.CompilerParams(vmem_limit_bytes=8 * 1024 * 1024),
        cost_estimate=pl.CostEstimate(flops=10**7, bytes_accessed=2**21, transcendentals=0),
        name="stage",
    )(increment, info)


def masked(piece, third, low_ref, high_ref):
    slots, depth = piece.shape
    column = lax.broadcasted_iota(jnp.int32, (slots, LANES), 1) // BLEV
    tiles = []
    for q in range(depth // LANES):
        r = column + COLS * q + third * (depth // BLEV)
        keep = (r >= low_ref[...]) & (r <= high_ref[...])
        part = piece[:, LANES * q : LANES * (q + 1)].astype(jnp.float32)
        tiles.append(jnp.where(keep, part, 0.0))
    return jnp.concatenate(tiles, axis=1)


def tile_product(jac_ref, prof_ref, s, t, base):
    row = prof_ref[s : s + 1, pl.ds(pl.multiple_of((t - base) * LANES, LANES), LANES)]
    tile = jac_ref[s, :, pl.ds(pl.multiple_of(t * LANES, LANES), LANES)]
    return tile.astype(jnp.float32) * row


def near_contract_kernel(info_ref, low_ref, high_ref, jac_ref, own_ref, near_ref, acc_ref, prof_ref):
    slots, depth = own_ref.shape
    odd = lax.rem(lax.axis_index("lon"), 2)
    start = pl.multiple_of((1 - odd) * depth, depth)
    prof_ref[:, pl.ds(pl.multiple_of(odd * depth, depth), depth)] = masked(
        own_ref[...], 1, low_ref, high_ref
    )
    prof_ref[:, pl.ds(start, depth)] = masked(near_ref[...], 2 - 2 * odd, low_ref, high_ref)
    zero = jnp.zeros(acc_ref.shape[1:], jnp.float32)
    base = 8 * (1 - odd)
    unroll, shift = 4, 4
    for s in range(slots):
        first = lax.max(info_ref[0, s], COLS * base)
        last = lax.min(info_ref[1, s], COLS * (base + 16) - 1)

        def step(g, total):
            for i in range(unroll):
                total = total + tile_product(jac_ref, prof_ref, s, unroll * g + i, base)
            return total

        acc_ref[s] = lax.fori_loop(
            lax.shift_right_arithmetic(first, shift), lax.shift_right_arithmetic(last, shift) + 1, step, zero
        )


def near_contract(info, low, high, jacobian, own, near):
    slots, depth = own.shape
    tangents = jacobian.shape[1]
    return pl.pallas_call(
        near_contract_kernel,
        out_shape=jax.ShapeDtypeStruct((slots, tangents, LANES), jnp.float32),
        in_specs=[SMEM] + [VMEM] * 5,
        out_specs=VMEM,
        scratch_shapes=[pltpu.VMEM((slots, 2 * depth), jnp.float32)],
        compiler_params=pltpu.CompilerParams(vmem_limit_bytes=20 * 1024 * 1024),
        cost_estimate=pl.CostEstimate(
            flops=4 * slots * tangents * depth, bytes_accessed=4 * slots * tangents * depth, transcendentals=0
        ),
        name="near_contract",
    )(info, low, high, jacobian, own, near)


def far_contract_kernel(low_ref, high_ref, jac_ref, far_ref, acc_ref, out_ref, prof_ref):
    slots, tangents = out_ref.shape
    odd = lax.rem(lax.axis_index("lon"), 2)
    base = 16 * odd
    prof_ref[...] = masked(far_ref[...], 2 * odd, low_ref, high_ref)
    place = lax.broadcasted_iota(jnp.int32, (tangents, LANES), 1)
    result = jnp.zeros((tangents, LANES), jnp.float32)
    for s in range(slots):
        total = acc_ref[s]
        for u in range(8):
            total = total + tile_product(jac_ref, prof_ref, s, base + u, base)
        result = jnp.where(place == s, jnp.sum(total, axis=1, keepdims=True), result)
    out_ref[...] = jnp.transpose(result)[:slots]


def far_contract(low, high, jacobian, far, acc):
    slots, depth = far.shape
    tangents = jacobian.shape[1]
    return pl.pallas_call(
        far_contract_kernel,
        out_shape=jax.ShapeDtypeStruct((slots, tangents), jnp.float32),
        in_specs=[VMEM] * 5,
        out_specs=VMEM,
        scratch_shapes=[pltpu.VMEM((slots, depth), jnp.float32)],
        compiler_params=pltpu.CompilerParams(vmem_limit_bytes=24 * 1024 * 1024),
        cost_estimate=pl.CostEstimate(
            flops=2 * slots * tangents * depth, bytes_accessed=2 * slots * tangents * depth, transcendentals=0
        ),
        name="far_contract",
    )(low, high, jacobian, far, acc)


def local(increment, jacobian, lat_weight, centre, west, east, lat_offset, lev_offset):
    n_lon, n_lat = lax.axis_size("lon"), lax.axis_size("lat")
    slots = centre.shape[0]

    def within(flip):
        return [(a * n_lat + b, a * n_lat + (b ^ flip)) for a in range(n_lon) for b in range(n_lat)]

    def swaps(start):
        pairs = [(a % n_lon, (a + 1) % n_lon) for a in range(start, n_lon, 2)]
        return pairs + [(b, a) for a, b in pairs]

    def across(value):
        return lax.ppermute(value, AXES, within(2))

    meta = jnp.concatenate(
        [lat_weight.T, lat_offset[None].astype(jnp.float32), lev_offset[None].astype(jnp.float32)], axis=0
    )
    meta = lax.optimization_barrier(jnp.pad(meta, ((0, BLAT - 2), (0, 0))))
    meta_y = across(meta)
    pair = lax.ppermute(increment, AXES, within(1))
    info = jnp.pad(jnp.stack([32 + centre - west, 32 + centre + east]), ((0, 6), (0, LANES - slots)))
    inc, info, low, high = stage(increment, info, slots)
    meta = lax.optimization_barrier(jnp.concatenate([meta, meta_y], axis=1))
    meta_far = lax.ppermute(meta, "lon", swaps(1))
    meta_near = lax.ppermute(meta, "lon", swaps(0))

    own, own_other, near, near_other = select(jnp.concatenate([meta, meta_near], axis=1), inc, pair)
    near_other = across(near_other)
    near = (near + near_other).astype(jnp.bfloat16)
    near = lax.ppermute(near, "lon", swaps(0))
    far, far_other = select(meta_far, inc, pair)
    far_other = across(far_other)
    own_other = across(own_other)
    own = (own + own_other).astype(jnp.bfloat16)
    far = (far + far_other).astype(jnp.bfloat16)
    far = lax.ppermute(far, "lon", swaps(1))
    acc = near_contract(info, low, high, jacobian, own, near)
    return far_contract(low, high, jacobian, far, acc)


def solution(mesh):
    return jax.shard_map(
        local,
        mesh=mesh,
        in_specs=(
            P("lon", "lat", None),
            P(("lon", "lat"), None, None),
            P(("lon", "lat"), None),
            P(("lon", "lat")),
            P(("lon", "lat")),
            P(("lon", "lat")),
            P(("lon", "lat")),
            P(("lon", "lat")),
        ),
        out_specs=P(("lon", "lat"), None),
        check_vma=False,
    )
```

time: 45.8 us -> 38.6 us (0.84)
  local copies, waits for them, and re-layouts: 7.11 us -> 1.25 us
  other arithmetic: 3.68 us -> 2.25 us
  waiting for transfers between devices: 6.33 us -> 7.57 us
  starting transfers between devices: 22 us -> 21.1 us
    unnamed x6 -> x8, local copies, waits for them, and re-layouts: 7.02 us -> 1.24 us
    ppermute x2, starting transfers between devices: 7.91 us -> 5.72 us  [the longest x1 5.63 us: local(): far = lax.ppermute(far, 'lon', swaps(1))]
    ppermute x1, waiting for transfers between devices: 0.01 us -> 2.02 us  [local(): meta_near = lax.ppermute(meta, 'lon', swaps(0))]
    ppermute x3 -> x4, starting transfers between devices: 4.36 us -> 5.7 us  [across(): return lax.ppermute(value, AXES, within(2))]
    ppermute x1, waiting for transfers between devices: 1.55 us -> 0.23 us  [local(): meta_far = lax.ppermute(meta, 'lon', swaps(1))]
    ppermute x2, waiting for transfers between devices: 3.14 us -> 3.88 us  [the longest x1 3.87 us: local(): near = lax.ppermute(near, 'lon', swaps(0))]
    concatenate x1, other arithmetic: 0.77 us -> 0.08 us  [local(): jnp.concatenate([meta, meta_near], axis=1)]
    concatenate x1, other arithmetic: 0.76 us -> 0.07 us  [local(): meta = lax.optimization_barrier(jnp.concatenate([meta, meta_y], axis=1))]
  transfers between devices with their start and end apart: 8 -> 9, of which waited for: 4 -> 5; matrix products, arithmetic and copies ran while one was open for 8% -> 6% of each run, Pallas kernels for 4% -> 9%
where the time goes in v2:
time: 38.6 us; the launch traced here: 38.5 us
  starting transfers between devices  21.1 us (55%)
  waiting for transfers between devices  7.57 us (20%)
  Pallas kernels  6.19 us (16%)
  other arithmetic  2.25 us (6%)
  local copies, waits for them, and re-layouts  1.25 us (3%)
    ppermute x1, starting transfers between devices, local(): meta_far = lax.ppermute(meta, 'lon', swaps(1))  9.67 us
    ppermute x4, starting transfers between devices, across(): return lax.ppermute(value, AXES, within(2))  5.7 us
    ppermute x1, starting transfers between devices, local(): far = lax.ppermute(far, 'lon', swaps(1))  5.63 us
    ppermute x1, waiting for transfers between devices, local(): near = lax.ppermute(near, 'lon', swaps(0))  3.87 us
    pallas_call x1, Pallas kernels, near_contract(): pl.pallas_call(near_contract_kernel, out_shape=jax.ShapeDtypeStruct((slot...  2.39 us
    ppermute x1, waiting for transfers between devices, local(): meta_near = lax.ppermute(meta, 'lon', swaps(0))  2.02 us
    pallas_call x1, Pallas kernels, far_contract(): pl.pallas_call(far_contract_kernel, out_shape=jax.ShapeDtypeStruct((slots...  1.97 us
    pallas_call x2, Pallas kernels, select(): pl.pallas_call(select_kernel, out_shape=(out,) * outs, in_specs=[VMEM] *...  1.68 us
  transfers between devices with their start and end apart: 9, of which 5 were waited for; matrix products, arithmetic and copies ran while one was open for 6% of the time, Pallas kernels for 9%

profile of v2, /device:TPU:8, one launch (start us, length us, event | category | flops | bytes accessed | tf_op | source)
XLA Modules:
  0.0 38.5 jit_solution(10603715035412906248)
XLA Ops:
  0.0 0.7 %convert_bitcast_fusion = (f32[1,16]{1,0:T(1,128)S(1)}, f32[1,16]{1,0:T(1,128)S(1)}) fusion(s32[16]{0:T(128)} %param.15, s32[16]{0:T(128)} %param.14), kind=kLoop, calls=%fused_computation.10 | loop fusion | flops 32 | bytes 256 | tf_op jit(solution)/shard_map/convert_element_type | solution.py:216
  0.7 0.7 %select_maximum_fusion.1 = f32[16,16]{1,0:T(8,128)S(1)} fusion(f32[1,16]{1,0:T(1,128)S(1)} %get-tuple-element.27, f32[1,16]{1,0:T(1,128)S(1)} %get-tuple-element.28, f32[8,16]{1,0:T(8,128)} %bitcast.11), kind=kLoop, calls=%fused_computation.5 | loop fusion | flops 1536 | bytes 1664 | tf_op jit(solution)/shard_map/concatenate | solution.py:215
  1.4 2.2 %collective-permute-start = (f32[16,16]{1,0:T(8,128)S(1)}, f32[16,16]{1,0:T(8,128)S(1)}, u32[]{:S(2)}, u32[]{:S(2)}) collective-permute-start(f32[16,16]{1,0:T(8,128)S(1)} %select_maximum_fusion.1), channel_id=1, source_target_pairs={{0,2},{1,3},{2,0},{3,1},{4,6},{5,7},{6,4},{7,5},{8,10},{9,11},{10,... | collective-permute-start | bytes 3080 | tf_op jit(solution)/shard_map/ppermute | solution.py:213
  3.5 0.7 %subtract_bitcast_fusion = (s32[1,16]{1,0:T(1,128)S(1)}, s32[1,16]{1,0:T(1,128)S(1)}) fusion(s32[16]{0:T(128)} %param.12, s32[16]{0:T(128)} %param.11, s32[16]{0:T(128)} %param.13), kind=kLoop, calls=%fused_computation.13 | loop fusion | flops 48 | bytes 320 | tf_op jit(solution)/shard_map/stack | solution.py:221
  4.2 0.9 %collective-permute-done = f32[16,16]{1,0:T(8,128)S(1)} collective-permute-done((f32[16,16]{1,0:T(8,128)S(1)}, f32[16,16]{1,0:T(8,128)S(1)}, u32[]{:S(2)}, u32[]{:S(2)}) %collective-permute-start) | collective-permute-done | bytes 1056 | tf_op jit(solution)/shard_map/ppermute | solution.py:213
  5.2 0.1 pad_maximum_fusion
  5.2 9.7 %collective-permute-start.1 = (f32[16,32]{1,0:T(8,128)S(1)}, f32[16,32]{1,0:T(8,128)S(1)}, u32[]{:S(2)}, u32[]{:S(2)}) collective-permute-start(f32[16,32]{1,0:T(8,128)S(1)} %pad_maximum_fusion), channel_id=1, source_target_pairs={{4,8},{12,16},{20,24},{28,32},{36,40},{44,48},{52,56},{60,64},{68,... | collective-permute-start | bytes 6152 | tf_op jit(solution)/shard_map/ppermute | solution.py:224
  14.9 1.2 %copy-done = bf16[32,128,128]{2,1,0:T(8,128)(2,1)S(1)} copy-done((bf16[32,128,128]{2,1,0:T(8,128)(2,1)S(1)}, bf16[32,128,128]{2,1,0:T(8,128)(2,1)}, u32[]{:S(2)}) %copy-start) | copy-done | bytes 1048600
  16.2 0.1 stage.1
  16.3 0.2 collective-permute-done.1
  16.5 2.0 %collective-permute-done.5 = f32[16,32]{1,0:T(8,128)S(1)} collective-permute-done((f32[16,32]{1,0:T(8,128)S(1)}, f32[16,32]{1,0:T(8,128)S(1)}, u32[]{:S(2)}, u32[]{:S(2)}) %collective-permute-start.5) | collective-permute-done | bytes 2080 | tf_op jit(solution)/shard_map/ppermute | solution.py:225
  18.6 0.1 select_maximum_fusion.meta_ref
  18.6 0.7 %shard_map.82 = (f32[16,1024]{1,0:T(8,128)S(1)}, f32[16,1024]{1,0:T(8,128)S(1)}) custom-call(f32[16,128]{1,0:T(8,128)S(1)} %pad.18.meta_ref, bf16[32,128,128]{2,1,0:T(8,128)(2,1)S(1)} %get-tuple-element.17.own_ref, bf16[32,128,128]{2,1,0:T(8,128)(2,1)S(1)} %collective-permute-done.2.pair_ref), custom_call_target="tpu_custom_call" | custom-call | flops 5000000000 | bytes 2097152 | tf_op jit(solution)/shard_map/pallas_call | solution.py:70
  19.4 0.0 slice-start.2
  19.4 1.4 %collective-permute-start.3 = (f32[16,1024]{1,0:T(8,128)S(1)}, f32[16,1024]{1,0:T(8,128)S(1)}, u32[]{:S(2)}, u32[]{:S(2)}) collective-permute-start(f32[16,1024]{1,0:T(8,128)S(1)} %get-tuple-element.19), channel_id=1, source_target_pairs={{0,2},{1,3},{2,0},{3,1},{4,6},{5,7},{6,4},{7,5},{8,10},{9,11},{10,... | collective-permute-start | bytes 196616 | tf_op jit(solution)/shard_map/ppermute | solution.py:213
  20.8 1.0 %shard_map.83 = (f32[16,1024]{1,0:T(8,128)S(1)}, f32[16,1024]{1,0:T(8,128)S(1)}, f32[16,1024]{1,0:T(8,128)S(1)}, f32[16,1024]{1,0:T(8,128)S(1)}) custom-call(f32[16,128]{1,0:T(8,128)S(1)} %select_maximum_fusion.meta_ref, bf16[32,128,128]{2,1,0:T(8,128)(2,1)S(1)} %get-tuple-element.17.own_ref, bf16[32,128,128]{2,1,0:T(8,128)(2,1)S(1)} %collective-permute-done.2.pair_ref), custom_call_target="tpu_custom_call" | custom-call | flops 5000000000 | bytes 2097152 | tf_op jit(solution)/shard_map/pallas_call | solution.py:70
  21.8 0.8 %collective-permute-start.6 = (f32[16,1024]{1,0:T(8,128)S(1)}, f32[16,1024]{1,0:T(8,128)S(1)}, u32[]{:S(2)}, u32[]{:S(2)}) collective-permute-start(f32[16,1024]{1,0:T(8,128)S(1)} %get-tuple-element.22), channel_id=1, source_target_pairs={{0,2},{1,3},{2,0},{3,1},{4,6},{5,7},{6,4},{7,5},{8,10},{9,11},{10,... | collective-permute-start | bytes 196616 | tf_op jit(solution)/shard_map/ppermute | solution.py:213
  22.6 1.3 %collective-permute-start.7 = (f32[16,1024]{1,0:T(8,128)S(1)}, f32[16,1024]{1,0:T(8,128)S(1)}, u32[]{:S(2)}, u32[]{:S(2)}) collective-permute-start(f32[16,1024]{1,0:T(8,128)S(1)} %get-tuple-element.24), channel_id=1, source_target_pairs={{0,2},{1,3},{2,0},{3,1},{4,6},{5,7},{6,4},{7,5},{8,10},{9,11},{10,... | collective-permute-start | bytes 196616 | tf_op jit(solution)/shard_map/ppermute | solution.py:213
  23.9 0.5 %collective-permute-done.3 = f32[16,1024]{1,0:T(8,128)S(1)} collective-permute-done((f32[16,1024]{1,0:T(8,128)S(1)}, f32[16,1024]{1,0:T(8,128)S(1)}, u32[]{:S(2)}, u32[]{:S(2)}) %collective-permute-start.3) | collective-permute-done | bytes 65568 | tf_op jit(solution)/shard_map/ppermute | solution.py:213
  24.4 5.6 %collective-permute-start.4 = (bf16[16,1024]{1,0:T(8,128)(2,1)S(1)}, bf16[16,1024]{1,0:T(8,128)(2,1)S(1)}, u32[]{:S(2)}, u32[]{:S(2)}) collective-permute-start(bf16[16,1024]{1,0:T(8,128)(2,1)S(1)} %add_convert_fusion.2), channel_id=1, source_target_pairs={{4,8},{12,16},{20,24},{28,32},{36,40},{44,48},{52,56},{60,64},{68,... | collective-permute-start | bytes 98312 | tf_op jit(solution)/shard_map/ppermute | solution.py:236
  30.1 0.1 collective-permute-start.8
  30.2 3.9 %collective-permute-done.8.near_ref = bf16[16,1024]{1,0:T(8,128)(2,1)S(1)} collective-permute-done((bf16[16,1024]{1,0:T(8,128)(2,1)S(1)}, bf16[16,1024]{1,0:T(8,128)(2,1)S(1)}, u32[]{:S(2)}, u32[]{:S(2)}) %collective-permute-start.8) | collective-permute-done | bytes 32800 | tf_op jit(solution)/shard_map/ppermute | solution.py:230
  34.1 2.4 %near_contract.1.acc_ref = f32[16,128,128]{2,1,0:T(8,128)S(1)} custom-call(s32[8,128]{1,0:T(8,128)S(1)} %get-tuple-element.20.info_ref, s32[16,128]{1,0:T(8,128)S(1)} %get-tuple-element.15.low_ref, s32[16,128]{1,0:T(8,128)S(1)} %get-tuple-element.16.high_ref, bf16[16,128,3072]{2,1,0:T(8,128)(2,1)S(1)} %bitcast.10, ...), custom_call_target="tpu_custom_call" | custom-call | flops 8388608 | bytes 8388608 | tf_op jit(solution)/shard_map/near_contract/pallas_call | solution.py:155
  36.5 2.0 %far_contract.1 = f32[16,128]{1,0:T(8,128)} custom-call(s32[16,128]{1,0:T(8,128)S(1)} %get-tuple-element.15.low_ref, s32[16,128]{1,0:T(8,128)S(1)} %get-tuple-element.16.high_ref, bf16[16,128,3072]{2,1,0:T(8,128)(2,1)S(1)} %bitcast.10, bf16[16,1024]{1,0:T(8,128)(2,1)S(1)} %collective-permute-done.4.far_ref, f32[16,128,128]{2,1,0:T(8,128)S(1)} %near_contract.1.acc_ref), custom_call_target="tpu_custom_call" | custom-call | flops 4194304 | bytes 4194304 | tf_op jit(solution)/shard_map/far_contract/pallas_call | solution.py:187
  (19 shorter events, 0.1 us)
Async XLA Ops:
  0.0 18.6 %collective-permute-start.2 = (bf16[32,128,128]{2,1,0:T(8,128)(2,1)}, bf16[32,128,128]{2,1,0:T(8,128)(2,1)S(1)}, u32[]{:S(2)}, u32[]{:S(2)}) collective-permute-start(bf16[32,128,128]{2,1,0:T(8,128)(2,1)} %own_ref.1), channel_id=1, source_target_pairs={{0,1},{1,0},{2,3},{3,2},{4,5},{5,4},{6,7},{7,6},{8,9},{9,8},{10,11... | collective-permute-start | bytes 3145736 | tf_op jit(solution)/shard_map/ppermute | solution.py:220
  1.4 3.8 %collective-permute-start = (f32[16,16]{1,0:T(8,128)S(1)}, f32[16,16]{1,0:T(8,128)S(1)}, u32[]{:S(2)}, u32[]{:S(2)}) collective-permute-start(f32[16,16]{1,0:T(8,128)S(1)} %select_maximum_fusion.1), channel_id=1, source_target_pairs={{0,2},{1,3},{2,0},{3,1},{4,6},{5,7},{6,4},{7,5},{8,10},{9,11},{10,... | collective-permute-start | bytes 3080 | tf_op jit(solution)/shard_map/ppermute | solution.py:213
  5.2 11.3 %collective-permute-start.1 = (f32[16,32]{1,0:T(8,128)S(1)}, f32[16,32]{1,0:T(8,128)S(1)}, u32[]{:S(2)}, u32[]{:S(2)}) collective-permute-start(f32[16,32]{1,0:T(8,128)S(1)} %pad_maximum_fusion), channel_id=1, source_target_pairs={{4,8},{12,16},{20,24},{28,32},{36,40},{44,48},{52,56},{60,64},{68,... | collective-permute-start | bytes 6152 | tf_op jit(solution)/shard_map/ppermute | solution.py:224
  14.9 3.7 %collective-permute-start.5 = (f32[16,32]{1,0:T(8,128)S(1)}, f32[16,32]{1,0:T(8,128)S(1)}, u32[]{:S(2)}, u32[]{:S(2)}) collective-permute-start(f32[16,32]{1,0:T(8,128)S(1)} %pad_maximum_fusion), channel_id=1, source_target_pairs={{0,4},{8,12},{16,20},{24,28},{32,36},{40,44},{48,52},{56,60},{64,6... | collective-permute-start | bytes 6152 | tf_op jit(solution)/shard_map/ppermute | solution.py:225
  14.9 1.2 %copy-start = (bf16[32,128,128]{2,1,0:T(8,128)(2,1)S(1)}, bf16[32,128,128]{2,1,0:T(8,128)(2,1)}, u32[]{:S(2)}) copy-start(bf16[32,128,128]{2,1,0:T(8,128)(2,1)} %own_ref.1) | copy-start | bytes 3145732
  18.6 15.4 %slice-start = ((s8[12582912]{0:T(1024)(128)(4,1)}), s8[4194304]{0:T(1024)(128)(4,1)S(1)}, s32[]{:S(2)}) async-start(s8[12582912]{0:T(1024)(128)(4,1)} %bitcast.9), calls=%async_computation | async-start | bytes 8388608
  18.6 15.4 %slice-start.1 = ((s8[12582912]{0:T(1024)(128)(4,1)}), s8[4194304]{0:T(1024)(128)(4,1)S(1)}, s32[]{:S(2)}) async-start(s8[12582912]{0:T(1024)(128)(4,1)} %bitcast.9), calls=%async_computation.1 | async-start | bytes 8388608
  19.4 14.7 %slice-start.2 = ((s8[12582912]{0:T(1024)(128)(4,1)}), s8[4194304]{0:T(1024)(128)(4,1)S(1)}, s32[]{:S(2)}) async-start(s8[12582912]{0:T(1024)(128)(4,1)} %bitcast.9), calls=%async_computation.2 | async-start | bytes 8388608
  19.4 5.0 %collective-permute-start.3 = (f32[16,1024]{1,0:T(8,128)S(1)}, f32[16,1024]{1,0:T(8,128)S(1)}, u32[]{:S(2)}, u32[]{:S(2)}) collective-permute-start(f32[16,1024]{1,0:T(8,128)S(1)} %get-tuple-element.19), channel_id=1, source_target_pairs={{0,2},{1,3},{2,0},{3,1},{4,6},{5,7},{6,4},{7,5},{8,10},{9,11},{10,... | collective-permute-start | bytes 196616 | tf_op jit(solution)/shard_map/ppermute | solution.py:213
  21.8 8.4 %collective-permute-start.6 = (f32[16,1024]{1,0:T(8,128)S(1)}, f32[16,1024]{1,0:T(8,128)S(1)}, u32[]{:S(2)}, u32[]{:S(2)}) collective-permute-start(f32[16,1024]{1,0:T(8,128)S(1)} %get-tuple-element.22), channel_id=1, source_target_pairs={{0,2},{1,3},{2,0},{3,1},{4,6},{5,7},{6,4},{7,5},{8,10},{9,11},{10,... | collective-permute-start | bytes 196616 | tf_op jit(solution)/shard_map/ppermute | solution.py:213
  22.6 7.5 %collective-permute-start.7 = (f32[16,1024]{1,0:T(8,128)S(1)}, f32[16,1024]{1,0:T(8,128)S(1)}, u32[]{:S(2)}, u32[]{:S(2)}) collective-permute-start(f32[16,1024]{1,0:T(8,128)S(1)} %get-tuple-element.24), channel_id=1, source_target_pairs={{0,2},{1,3},{2,0},{3,1},{4,6},{5,7},{6,4},{7,5},{8,10},{9,11},{10,... | collective-permute-start | bytes 196616 | tf_op jit(solution)/shard_map/ppermute | solution.py:213
  24.4 12.1 %collective-permute-start.4 = (bf16[16,1024]{1,0:T(8,128)(2,1)S(1)}, bf16[16,1024]{1,0:T(8,128)(2,1)S(1)}, u32[]{:S(2)}, u32[]{:S(2)}) collective-permute-start(bf16[16,1024]{1,0:T(8,128)(2,1)S(1)} %add_convert_fusion.2), channel_id=1, source_target_pairs={{4,8},{12,16},{20,24},{28,32},{36,40},{44,48},{52,56},{60,64},{68,... | collective-permute-start | bytes 98312 | tf_op jit(solution)/shard_map/ppermute | solution.py:236
  30.1 4.0 %collective-permute-start.8 = (bf16[16,1024]{1,0:T(8,128)(2,1)S(1)}, bf16[16,1024]{1,0:T(8,128)(2,1)S(1)}, u32[]{:S(2)}, u32[]{:S(2)}) collective-permute-start(bf16[16,1024]{1,0:T(8,128)(2,1)S(1)} %add_convert_fusion), channel_id=1, source_target_pairs={{0,4},{8,12},{16,20},{24,28},{32,36},{40,44},{48,52},{56,60},{64,6... | collective-permute-start | bytes 98312 | tf_op jit(solution)/shard_map/ppermute | solution.py:230

commit v3 on v2

v3 whole, which is shorter than its diff:
```python
import functools

import jax
import jax.numpy as jnp
from jax import lax
from jax.experimental import pallas as pl
from jax.experimental.pallas import tpu as pltpu
from jax.sharding import PartitionSpec as P


BLAT = 8
BLEV = 32
LANES = 128
COLS = LANES // BLEV
AXES = ("lon", "lat")
VMEM = pl.BlockSpec(memory_space=pltpu.VMEM)


def select_kernel(keep, meta_ref, own_ref, pair_ref, *outs):
    if keep:
        outs[-1][...] = own_ref[...]
        outs = outs[:-1]
    width, rows = own_ref.shape[0], own_ref.shape[1]
    groups = len(outs) // 2
    count = 32 * groups
    meta = jnp.transpose(meta_ref[...])[:count]
    band = lax.axis_index("lat")
    lat_first, lev_first = [meta[:, BLAT + i : BLAT + i + 1].astype(jnp.int32) for i in range(2)]
    lane = lax.broadcasted_iota(jnp.int32, (count, LANES), 1)

    def weights(first):
        offset = lane + first - lat_first
        total = jnp.zeros((count, LANES), jnp.float32)
        for j in range(BLAT):
            total = jnp.where(offset == j, meta[:, j : j + 1], total)
        return total

    full = jnp.concatenate(
        [weights(band * rows), weights((band + 1 - 2 * lax.rem(band, 2)) * rows)], axis=1
    )
    high = full.astype(jnp.bfloat16)
    low = (full - high.astype(jnp.float32)).astype(jnp.bfloat16)
    left = jnp.concatenate([high, low], axis=0)
    index = lev_first + lax.rem(lane, BLEV)
    spot = lane // BLEV
    for q in range(width // COLS):
        tile = None
        for h in range(COLS // 2):
            c = COLS * q + 2 * h
            right = jnp.concatenate(
                [
                    jnp.concatenate([own_ref[c], pair_ref[c]], axis=0),
                    jnp.concatenate([own_ref[c + 1], pair_ref[c + 1]], axis=0),
                ],
                axis=1,
            )
            both = jnp.dot(left, right, preferred_element_type=jnp.float32)
            both = both[:count] + both[count:]
            for i in range(2):
                box = jnp.take_along_axis(both[:, LANES * i : LANES * (i + 1)], index, axis=1)
                tile = box if tile is None else jnp.where(spot == 2 * h + i, box, tile)
        at = slice(LANES * q, LANES * (q + 1))
        for g in range(groups):
            outs[2 * g][:, at] = tile[32 * g : 32 * g + 16]
            outs[2 * g + 1][:, at] = tile[32 * g + 16 : 32 * g + 32]


def select(meta, own, pair, keep):
    count = meta.shape[1]
    width = own.shape[0]
    meta = jnp.pad(meta, ((0, 0), (0, LANES - count)))
    out = jax.ShapeDtypeStruct((16, width * BLEV), jnp.float32)
    outs = (out,) * (count // 16)
    if keep:
        outs += (jax.ShapeDtypeStruct(own.shape, own.dtype),)
    return pl.pallas_call(
        functools.partial(select_kernel, keep),
        out_shape=outs,
        in_specs=[VMEM] * 3,
        out_specs=(VMEM,) * len(outs),
        compiler_params=pltpu.CompilerParams(vmem_limit_bytes=12 * 1024 * 1024),
        cost_estimate=pl.CostEstimate(
            flops=5 * 10**9, bytes_accessed=2 * 1024 * 1024, transcendentals=0
        ),
    )(meta, own, pair)


def limits_kernel(info_ref, low_out, high_out):
    slots = low_out.shape[0]
    bounds = jnp.transpose(info_ref[...])[:slots]
    low_out[...] = jnp.broadcast_to(bounds[:, :1], low_out.shape)
    high_out[...] = jnp.broadcast_to(bounds[:, 1:2], high_out.shape)


def limits(info, slots):
    bound = jax.ShapeDtypeStruct((slots, LANES), info.dtype)
    return pl.pallas_call(
        limits_kernel,
        out_shape=(bound, bound),
        in_specs=[VMEM],
        out_specs=(VMEM, VMEM),
        compiler_params=pltpu.CompilerParams(vmem_limit_bytes=4 * 1024 * 1024),
        name="limits",
    )(info)


def mark_kernel(meta_ref, out_ref):
    out_ref[...] = meta_ref[...]


def mark(meta):
    return pl.pallas_call(
        mark_kernel,
        out_shape=jax.ShapeDtypeStruct(meta.shape, meta.dtype),
        in_specs=[VMEM],
        out_specs=VMEM,
        compiler_params=pltpu.CompilerParams(vmem_limit_bytes=4 * 1024 * 1024),
        cost_estimate=pl.CostEstimate(flops=5 * 10**9, bytes_accessed=2**14, transcendentals=0),
        name="mark",
    )(meta)


def masked(piece, third, low_ref, high_ref):
    slots, depth = piece.shape
    column = lax.broadcasted_iota(jnp.int32, (slots, LANES), 1) // BLEV
    tiles = []
    for q in range(depth // LANES):
        r = column + COLS * q + third * (depth // BLEV)
        keep = (r >= low_ref[...]) & (r <= high_ref[...])
        part = piece[:, LANES * q : LANES * (q + 1)].astype(jnp.float32)
        tiles.append(jnp.where(keep, part, 0.0).astype(jnp.bfloat16))
    return jnp.concatenate(tiles, axis=1)


def scan_rows(jac_ref, profile, third, start):
    slots, depth = profile.shape
    row = lax.broadcasted_iota(jnp.int32, start.shape, 0)
    at = pl.ds(pl.multiple_of(third * depth, depth), depth)
    rows = start
    for s in range(slots):
        product = lax.dot_general(
            profile, jac_ref[s, :, at], (((1,), (1,)), ((), ())), preferred_element_type=jnp.float32
        )
        rows = jnp.where(row == s, rows + product, rows)
    return rows


def near_contract_kernel(low_ref, high_ref, jac_ref, own_ref, near_ref, part_ref):
    odd = lax.rem(lax.axis_index("lon"), 2)
    rows = jnp.zeros(part_ref.shape, jnp.float32)
    for piece, third in ((own_ref, 1), (near_ref, 2 - 2 * odd)):
        profile = masked(piece[...], third, low_ref, high_ref)
        rows = scan_rows(jac_ref, profile, third, rows)
    part_ref[...] = rows


def far_contract_kernel(low_ref, high_ref, jac_ref, far_ref, part_ref, out_ref):
    third = 2 * lax.rem(lax.axis_index("lon"), 2)
    profile = masked(far_ref[...], third, low_ref, high_ref)
    out_ref[...] = scan_rows(jac_ref, profile, third, part_ref[...])


def contract(kernel, jacobian, *operands):
    slots, tangents, depth = jacobian.shape
    return pl.pallas_call(
        kernel,
        out_shape=jax.ShapeDtypeStruct((slots, tangents), jnp.float32),
        in_specs=[VMEM] * (1 + len(operands)),
        out_specs=VMEM,
        compiler_params=pltpu.CompilerParams(vmem_limit_bytes=20 * 1024 * 1024),
        cost_estimate=pl.CostEstimate(
            flops=4 * slots * tangents * depth, bytes_accessed=4 * slots * tangents * depth, transcendentals=0
        ),
    )(*operands[:2], jacobian, *operands[2:])


def local(increment, jacobian, lat_weight, centre, west, east, lat_offset, lev_offset):
    n_lon, n_lat = lax.axis_size("lon"), lax.axis_size("lat")
    slots = centre.shape[0]

    def within(flip):
        return [(a * n_lat + b, a * n_lat + (b ^ flip)) for a in range(n_lon) for b in range(n_lat)]

    def swaps(start):
        pairs = [(a % n_lon, (a + 1) % n_lon) for a in range(start, n_lon, 2)]
        return pairs + [(b, a) for a, b in pairs]

    def crossed(start, flip):
        return [(a * n_lat + b, c * n_lat + (b ^ flip)) for a, c in swaps(start) for b in range(n_lat)]

    def across(value):
        return lax.ppermute(value, AXES, within(2))

    meta = jnp.concatenate(
        [lat_weight.T, lat_offset[None].astype(jnp.float32), lev_offset[None].astype(jnp.float32)], axis=0
    )
    meta = mark(jnp.pad(meta, ((0, BLAT - 2), (0, 0))))
    meta_y = across(meta)
    near_a = lax.ppermute(meta, AXES, crossed(0, 0))
    near_b = lax.ppermute(meta, AXES, crossed(0, 2))
    pair = lax.ppermute(increment, AXES, within(1))
    meta = lax.optimization_barrier(jnp.concatenate([meta, meta_y], axis=1))
    meta_far = lax.ppermute(meta, "lon", swaps(1))

    own, own_other, near, near_other, inc = select(
        jnp.concatenate([meta, near_a, near_b], axis=1), increment, pair, True
    )
    near_other = across(near_other)
    near = (near + near_other).astype(jnp.bfloat16)
    near = lax.ppermute(near, "lon", swaps(0))
    far, far_other = select(meta_far, inc, pair, False)
    far_other = across(far_other)
    info = jnp.pad(jnp.stack([32 + centre - west, 32 + centre + east]), ((0, 6), (0, LANES - slots)))
    low, high = limits(info, slots)
    own_other = across(own_other)
    own = (own + own_other).astype(jnp.bfloat16)
    far = (far + far_other).astype(jnp.bfloat16)
    far = lax.ppermute(far, "lon", swaps(1))
    part = contract(near_contract_kernel, jacobian, low, high, own, near)
    return contract(far_contract_kernel, jacobian, low, high, far, part)


def solution(mesh):
    return jax.shard_map(
        local,
        mesh=mesh,
        in_specs=(
            P("lon", "lat", None),
            P(("lon", "lat"), None, None),
            P(("lon", "lat"), None),
            P(("lon", "lat")),
            P(("lon", "lat")),
            P(("lon", "lat")),
            P(("lon", "lat")),
            P(("lon", "lat")),
        ),
        out_specs=P(("lon", "lat"), None),
        check_vma=False,
    )
```

time: 38.6 us -> 37.2 us (0.964)
  starting transfers between devices: 21.1 us -> 25 us
  waiting for transfers between devices: 7.57 us -> 4.39 us
  local copies, waits for them, and re-layouts: 1.25 us -> 0.04 us
  other arithmetic: 2.25 us -> 1.66 us
    ppermute x1, waiting for transfers between devices: 3.87 us -> 0.01 us  [local(): near = lax.ppermute(near, 'lon', swaps(0))]
    ppermute x1, starting transfers between devices: 5.63 us -> 7.83 us  [local(): far = lax.ppermute(far, 'lon', swaps(1))]
    ppermute x1 -> x2, waiting for transfers between devices: 2.02 us -> 0.01 us  [the longest x1 0.01 us: local(): near_a = lax.ppermute(meta, AXES, crossed(0, 0))]
    ppermute x1 -> x2, starting transfers between devices: 0.01 us -> 1.56 us  [the longest x1 1.34 us: local(): near_b = lax.ppermute(meta, AXES, crossed(0, 2))]
    ppermute x4, waiting for transfers between devices: 1.44 us -> 2.8 us  [across(): return lax.ppermute(value, AXES, within(2))]
    ppermute x1, waiting for transfers between devices: 0.23 us -> 1.55 us  [local(): meta_far = lax.ppermute(meta, 'lon', swaps(1))]
    unnamed x8 -> x14, local copies, waits for them, and re-layouts: 1.24 us -> 0.03 us
    another operation x2, other arithmetic: 0.7 us -> 0.01 us  [local(): jnp.stack([32 + centre - west, 32 + centre + east])]
  transfers between devices with their start and end apart: 9 -> 10, of which waited for: 5 -> 3; matrix products, arithmetic and copies ran while one was open for 6% -> 4% of each run, Pallas kernels for 9% -> 8%
where the time goes in v3:
time: 37.2 us; the launch traced here: 37.1 us
  starting transfers between devices  25 us (67%)
  Pallas kernels  5.91 us (16%)
  waiting for transfers between devices  4.39 us (12%)
  other arithmetic  1.66 us (4%)
    ppermute x1, starting transfers between devices, local(): meta_far = lax.ppermute(meta, 'lon', swaps(1))  9.59 us
    ppermute x1, starting transfers between devices, local(): far = lax.ppermute(far, 'lon', swaps(1))  7.83 us
    ppermute x4, starting transfers between devices, across(): return lax.ppermute(value, AXES, within(2))  5.78 us
    pallas_call x2, Pallas kernels, contract(): pl.pallas_call(kernel, out_shape=jax.ShapeDtypeStruct((slots, tangents),...  4.08 us
    ppermute x4, waiting for transfers between devices, across(): return lax.ppermute(value, AXES, within(2))  2.8 us
    pallas_call x2, Pallas kernels, select(): pl.pallas_call(functools.partial(select_kernel, keep), out_shape=outs, in...  1.71 us
    ppermute x1, waiting for transfers between devices, local(): meta_far = lax.ppermute(meta, 'lon', swaps(1))  1.55 us
    ppermute x1, starting transfers between devices, local(): near_b = lax.ppermute(meta, AXES, crossed(0, 2))  1.34 us
  transfers between devices with their start and end apart: 10, of which 3 were waited for; matrix products, arithmetic and copies ran while one was open for 4% of the time, Pallas kernels for 8%

profile of v3, /device:TPU:8, one launch (start us, length us, event | category | flops | bytes accessed | tf_op | source)
XLA Modules:
  0.0 37.1 jit_solution(9165900476897180109)
XLA Ops:
  0.0 0.1 collective-permute-start.4
  0.1 0.7 %convert_bitcast_fusion = (f32[1,16]{1,0:T(1,128)S(1)}, f32[1,16]{1,0:T(1,128)S(1)}) fusion(s32[16]{0:T(128)} %param.15, s32[16]{0:T(128)} %param.14), kind=kLoop, calls=%fused_computation.11 | loop fusion | flops 32 | bytes 256 | tf_op jit(solution)/shard_map/convert_element_type | solution.py:195
  0.9 0.7 %select_maximum_fusion.2.meta_ref = f32[16,16]{1,0:T(8,128)S(1)} fusion(f32[1,16]{1,0:T(1,128)S(1)} %get-tuple-element.25, f32[1,16]{1,0:T(1,128)S(1)} %get-tuple-element.26, f32[8,16]{1,0:T(8,128)} %bitcast.11), kind=kLoop, calls=%fused_computation.6 | loop fusion | flops 1536 | bytes 1664 | tf_op jit(solution)/shard_map/concatenate | solution.py:194
  1.6 2.2 %collective-permute-start = (f32[16,16]{1,0:T(8,128)S(1)}, f32[16,16]{1,0:T(8,128)S(1)}, u32[]{:S(2)}, u32[]{:S(2)}) collective-permute-start(f32[16,16]{1,0:T(8,128)S(1)} %mark.1), channel_id=1, source_target_pairs={{0,2},{1,3},{2,0},{3,1},{4,6},{5,7},{6,4},{7,5},{8,10},{9,11},{10,... | collective-permute-start | bytes 3080 | tf_op jit(solution)/shard_map/ppermute | solution.py:192
  3.8 0.2 collective-permute-start.2
  4.0 1.3 %collective-permute-start.3 = (f32[16,16]{1,0:T(8,128)S(1)}, f32[16,16]{1,0:T(8,128)S(1)}, u32[]{:S(2)}, u32[]{:S(2)}) collective-permute-start(f32[16,16]{1,0:T(8,128)S(1)} %mark.1), channel_id=1, source_target_pairs={{0,6},{1,7},{2,4},{3,5},{8,14},{9,15},{10,12},{11,13},{16,22},{17,... | collective-permute-start | bytes 3080 | tf_op jit(solution)/shard_map/ppermute | solution.py:200
  5.4 0.1 limits.1
  5.5 0.1 pad_maximum_fusion
  5.6 9.6 %collective-permute-start.1 = (f32[16,32]{1,0:T(8,128)S(1)}, f32[16,32]{1,0:T(8,128)S(1)}, u32[]{:S(2)}, u32[]{:S(2)}) collective-permute-start(f32[16,32]{1,0:T(8,128)S(1)} %pad_maximum_fusion), channel_id=1, source_target_pairs={{4,8},{12,16},{20,24},{28,32},{36,40},{44,48},{52,56},{60,64},{68,... | collective-permute-start | bytes 6152 | tf_op jit(solution)/shard_map/ppermute | solution.py:203
  15.2 0.1 select_maximum_fusion.meta_ref
  15.3 1.5 %collective-permute-done.1 = f32[16,32]{1,0:T(8,128)S(1)} collective-permute-done((f32[16,32]{1,0:T(8,128)S(1)}, f32[16,32]{1,0:T(8,128)S(1)}, u32[]{:S(2)}, u32[]{:S(2)}) %collective-permute-start.1) | collective-permute-done | bytes 2080 | tf_op jit(solution)/shard_map/ppermute | solution.py:203
  16.9 0.0 slice-start
  16.9 1.0 %shard_map.82 = (f32[16,1024]{1,0:T(8,128)S(1)}, f32[16,1024]{1,0:T(8,128)S(1)}, f32[16,1024]{1,0:T(8,128)S(1)}, f32[16,1024]{1,0:T(8,128)S(1)}, bf16[32,128,128]{2,1,0:T(8,128)(2,1)S(1)}) custom-call(f32[16,128]{1,0:T(8,128)S(1)} %select_maximum_fusion.meta_ref, bf16[32,128,128]{2,1,0:T(8,128)(2,1)S(1)} %copy-done, ...), custom_call_target="tpu_custom_call" | custom-call | flops 5000000000 | bytes 2097152 | tf_op jit(solution)/shard_map/pallas_call | solution.py:76
  17.9 1.4 %collective-permute-start.8 = (f32[16,1024]{1,0:T(8,128)S(1)}, f32[16,1024]{1,0:T(8,128)S(1)}, u32[]{:S(2)}, u32[]{:S(2)}) collective-permute-start(f32[16,1024]{1,0:T(8,128)S(1)} %get-tuple-element.22), channel_id=1, source_target_pairs={{0,2},{1,3},{2,0},{3,1},{4,6},{5,7},{6,4},{7,5},{8,10},{9,11},{10,... | collective-permute-start | bytes 196616 | tf_op jit(solution)/shard_map/ppermute | solution.py:192
  19.3 0.7 %collective-permute-start.7 = (f32[16,1024]{1,0:T(8,128)S(1)}, f32[16,1024]{1,0:T(8,128)S(1)}, u32[]{:S(2)}, u32[]{:S(2)}) collective-permute-start(f32[16,1024]{1,0:T(8,128)S(1)} %get-tuple-element.20), channel_id=1, source_target_pairs={{0,2},{1,3},{2,0},{3,1},{4,6},{5,7},{6,4},{7,5},{8,10},{9,11},{10,... | collective-permute-start | bytes 196616 | tf_op jit(solution)/shard_map/ppermute | solution.py:192
  20.0 0.7 %shard_map.83 = (f32[16,1024]{1,0:T(8,128)S(1)}, f32[16,1024]{1,0:T(8,128)S(1)}) custom-call(f32[16,128]{1,0:T(8,128)S(1)} %pad.18.meta_ref, bf16[32,128,128]{2,1,0:T(8,128)(2,1)S(1)} %get-tuple-element.16.own_ref, bf16[32,128,128]{2,1,0:T(8,128)(2,1)S(1)} %collective-permute-done.4.pair_ref), custom_call_target="tpu_custom_call" | custom-call | flops 5000000000 | bytes 2097152 | tf_op jit(solution)/shard_map/pallas_call | solution.py:76
  20.7 1.4 %collective-permute-start.5 = (f32[16,1024]{1,0:T(8,128)S(1)}, f32[16,1024]{1,0:T(8,128)S(1)}, u32[]{:S(2)}, u32[]{:S(2)}) collective-permute-start(f32[16,1024]{1,0:T(8,128)S(1)} %get-tuple-element.18), channel_id=1, source_target_pairs={{0,2},{1,3},{2,0},{3,1},{4,6},{5,7},{6,4},{7,5},{8,10},{9,11},{10,... | collective-permute-start | bytes 196616 | tf_op jit(solution)/shard_map/ppermute | solution.py:192
  22.2 0.7 %collective-permute-done.8 = f32[16,1024]{1,0:T(8,128)S(1)} collective-permute-done((f32[16,1024]{1,0:T(8,128)S(1)}, f32[16,1024]{1,0:T(8,128)S(1)}, u32[]{:S(2)}, u32[]{:S(2)}) %collective-permute-start.8) | collective-permute-done | bytes 65568 | tf_op jit(solution)/shard_map/ppermute | solution.py:192
  22.9 0.1 collective-permute-start.9
  23.0 2.1 %collective-permute-done.5 = f32[16,1024]{1,0:T(8,128)S(1)} collective-permute-done((f32[16,1024]{1,0:T(8,128)S(1)}, f32[16,1024]{1,0:T(8,128)S(1)}, u32[]{:S(2)}, u32[]{:S(2)}) %collective-permute-start.5) | collective-permute-done | bytes 65568 | tf_op jit(solution)/shard_map/ppermute | solution.py:192
  25.1 7.8 %collective-permute-start.6 = (bf16[16,1024]{1,0:T(8,128)(2,1)S(1)}, bf16[16,1024]{1,0:T(8,128)(2,1)S(1)}, u32[]{:S(2)}, u32[]{:S(2)}) collective-permute-start(bf16[16,1024]{1,0:T(8,128)(2,1)S(1)} %add_convert_fusion.2), channel_id=1, source_target_pairs={{4,8},{12,16},{20,24},{28,32},{36,40},{44,48},{52,56},{60,64},{68,... | collective-permute-start | bytes 98312 | tf_op jit(solution)/shard_map/ppermute | solution.py:218
  33.0 2.2 %shard_map.84.part_ref = f32[16,128]{1,0:T(8,128)S(1)} custom-call(s32[16,128]{1,0:T(8,128)S(1)} %get-tuple-element.14.low_ref, s32[16,128]{1,0:T(8,128)S(1)} %get-tuple-element.15.high_ref, bf16[16,128,3072]{2,1,0:T(8,128)(2,1)S(1)} %bitcast.10, bf16[16,1024]{1,0:T(8,128)(2,1)S(1)} %add_convert_fusion.1.own_ref, ...), custom_call_target="tpu_custom_call" | custom-call | flops 25165824 | bytes 25165824 | tf_op jit(solution)/shard_map/pallas_call | solution.py:165
  35.2 0.0 collective-permute-done.6.far_ref
  35.3 1.8 %shard_map.85 = f32[16,128]{1,0:T(8,128)} custom-call(s32[16,128]{1,0:T(8,128)S(1)} %get-tuple-element.14.low_ref, s32[16,128]{1,0:T(8,128)S(1)} %get-tuple-element.15.high_ref, bf16[16,128,3072]{2,1,0:T(8,128)(2,1)S(1)} %bitcast.10, bf16[16,1024]{1,0:T(8,128)(2,1)S(1)} %collective-permute-done.6.far_ref, f32[16,128]{1,0:T(8,128)S(1)} %shard_map.84.part_ref), custom_call_target="tpu_custom_call" | custom-call | flops 25165824 | bytes 25165824 | tf_op jit(solution)/shard_map/pallas_call | solution.py:165
  (28 shorter events, 0.1 us)
Async XLA Ops:
  0.0 16.9 %copy-start = (bf16[32,128,128]{2,1,0:T(8,128)(2,1)S(1)}, bf16[32,128,128]{2,1,0:T(8,128)(2,1)}, u32[]{:S(2)}) copy-start(bf16[32,128,128]{2,1,0:T(8,128)(2,1)} %own_ref.1) | copy-start | bytes 3145732
  0.0 5.4 %copy-start.2 = (s32[16]{0:T(128)S(1)}, s32[16]{0:T(128)}, u32[]{:S(2)}) copy-start(s32[16]{0:T(128)} %param.11) | copy-start | bytes 196
  0.0 5.4 %copy-start.1 = (s32[16]{0:T(128)S(1)}, s32[16]{0:T(128)}, u32[]{:S(2)}) copy-start(s32[16]{0:T(128)} %param.12) | copy-start | bytes 196
  0.0 5.4 %copy-start.3 = (s32[16]{0:T(128)S(1)}, s32[16]{0:T(128)}, u32[]{:S(2)}) copy-start(s32[16]{0:T(128)} %param.13) | copy-start | bytes 196
  0.0 16.8 %collective-permute-start.4 = (bf16[32,128,128]{2,1,0:T(8,128)(2,1)}, bf16[32,128,128]{2,1,0:T(8,128)(2,1)S(1)}, u32[]{:S(2)}, u32[]{:S(2)}) collective-permute-start(bf16[32,128,128]{2,1,0:T(8,128)(2,1)} %own_ref.1), channel_id=1, source_target_pairs={{0,1},{1,0},{2,3},{3,2},{4,5},{5,4},{6,7},{7,6},{8,9},{9,8},{10,11... | collective-permute-start | bytes 3145736 | tf_op jit(solution)/shard_map/ppermute | solution.py:201
  1.6 4.0 %collective-permute-start = (f32[16,16]{1,0:T(8,128)S(1)}, f32[16,16]{1,0:T(8,128)S(1)}, u32[]{:S(2)}, u32[]{:S(2)}) collective-permute-start(f32[16,16]{1,0:T(8,128)S(1)} %mark.1), channel_id=1, source_target_pairs={{0,2},{1,3},{2,0},{3,1},{4,6},{5,7},{6,4},{7,5},{8,10},{9,11},{10,... | collective-permute-start | bytes 3080 | tf_op jit(solution)/shard_map/ppermute | solution.py:192
  3.8 11.4 %collective-permute-start.2 = (f32[16,16]{1,0:T(8,128)S(1)}, f32[16,16]{1,0:T(8,128)S(1)}, u32[]{:S(2)}, u32[]{:S(2)}) collective-permute-start(f32[16,16]{1,0:T(8,128)S(1)} %mark.1), channel_id=1, source_target_pairs={{0,4},{1,5},{2,6},{3,7},{8,12},{9,13},{10,14},{11,15},{16,20},{17,... | collective-permute-start | bytes 3080 | tf_op jit(solution)/shard_map/ppermute | solution.py:199
  4.0 11.2 %collective-permute-start.3 = (f32[16,16]{1,0:T(8,128)S(1)}, f32[16,16]{1,0:T(8,128)S(1)}, u32[]{:S(2)}, u32[]{:S(2)}) collective-permute-start(f32[16,16]{1,0:T(8,128)S(1)} %mark.1), channel_id=1, source_target_pairs={{0,6},{1,7},{2,4},{3,5},{8,14},{9,15},{10,12},{11,13},{16,22},{17,... | collective-permute-start | bytes 3080 | tf_op jit(solution)/shard_map/ppermute | solution.py:200
  5.6 11.2 %collective-permute-start.1 = (f32[16,32]{1,0:T(8,128)S(1)}, f32[16,32]{1,0:T(8,128)S(1)}, u32[]{:S(2)}, u32[]{:S(2)}) collective-permute-start(f32[16,32]{1,0:T(8,128)S(1)} %pad_maximum_fusion), channel_id=1, source_target_pairs={{4,8},{12,16},{20,24},{28,32},{36,40},{44,48},{52,56},{60,64},{68,... | collective-permute-start | bytes 6152 | tf_op jit(solution)/shard_map/ppermute | solution.py:203
  16.9 16.1 %slice-start = ((s8[12582912]{0:T(1024)(128)(4,1)}), s8[4194304]{0:T(1024)(128)(4,1)S(1)}, s32[]{:S(2)}) async-start(s8[12582912]{0:T(1024)(128)(4,1)} %bitcast.9), calls=%async_computation | async-start | bytes 8388608
  16.9 16.1 %slice-start.1 = ((s8[12582912]{0:T(1024)(128)(4,1)}), s8[4194304]{0:T(1024)(128)(4,1)S(1)}, s32[]{:S(2)}) async-start(s8[12582912]{0:T(1024)(128)(4,1)} %bitcast.9), calls=%async_computation.1 | async-start | bytes 8388608
  17.9 5.0 %collective-permute-start.8 = (f32[16,1024]{1,0:T(8,128)S(1)}, f32[16,1024]{1,0:T(8,128)S(1)}, u32[]{:S(2)}, u32[]{:S(2)}) collective-permute-start(f32[16,1024]{1,0:T(8,128)S(1)} %get-tuple-element.22), channel_id=1, source_target_pairs={{0,2},{1,3},{2,0},{3,1},{4,6},{5,7},{6,4},{7,5},{8,10},{9,11},{10,... | collective-permute-start | bytes 196616 | tf_op jit(solution)/shard_map/ppermute | solution.py:192
  19.3 13.6 %collective-permute-start.7 = (f32[16,1024]{1,0:T(8,128)S(1)}, f32[16,1024]{1,0:T(8,128)S(1)}, u32[]{:S(2)}, u32[]{:S(2)}) collective-permute-start(f32[16,1024]{1,0:T(8,128)S(1)} %get-tuple-element.20), channel_id=1, source_target_pairs={{0,2},{1,3},{2,0},{3,1},{4,6},{5,7},{6,4},{7,5},{8,10},{9,11},{10,... | collective-permute-start | bytes 196616 | tf_op jit(solution)/shard_map/ppermute | solution.py:192
  20.0 13.0 %slice-start.2 = ((s8[12582912]{0:T(1024)(128)(4,1)}), s8[4194304]{0:T(1024)(128)(4,1)S(1)}, s32[]{:S(2)}) async-start(s8[12582912]{0:T(1024)(128)(4,1)} %bitcast.9), calls=%async_computation.2 | async-start | bytes 8388608
  20.7 4.4 %collective-permute-start.5 = (f32[16,1024]{1,0:T(8,128)S(1)}, f32[16,1024]{1,0:T(8,128)S(1)}, u32[]{:S(2)}, u32[]{:S(2)}) collective-permute-start(f32[16,1024]{1,0:T(8,128)S(1)} %get-tuple-element.18), channel_id=1, source_target_pairs={{0,2},{1,3},{2,0},{3,1},{4,6},{5,7},{6,4},{7,5},{8,10},{9,11},{10,... | collective-permute-start | bytes 196616 | tf_op jit(solution)/shard_map/ppermute | solution.py:192
  22.9 10.0 %collective-permute-start.9 = (bf16[16,1024]{1,0:T(8,128)(2,1)S(1)}, bf16[16,1024]{1,0:T(8,128)(2,1)S(1)}, u32[]{:S(2)}, u32[]{:S(2)}) collective-permute-start(bf16[16,1024]{1,0:T(8,128)(2,1)S(1)} %add_convert_fusion), channel_id=1, source_target_pairs={{0,4},{8,12},{16,20},{24,28},{32,36},{40,44},{48,52},{56,60},{64,6... | collective-permute-start | bytes 98312 | tf_op jit(solution)/shard_map/ppermute | solution.py:210
  25.1 10.2 %collective-permute-start.6 = (bf16[16,1024]{1,0:T(8,128)(2,1)S(1)}, bf16[16,1024]{1,0:T(8,128)(2,1)S(1)}, u32[]{:S(2)}, u32[]{:S(2)}) collective-permute-start(bf16[16,1024]{1,0:T(8,128)(2,1)S(1)} %add_convert_fusion.2), channel_id=1, source_target_pairs={{4,8},{12,16},{20,24},{28,32},{36,40},{44,48},{52,56},{60,64},{68,... | collective-permute-start | bytes 98312 | tf_op jit(solution)/shard_map/ppermute | solution.py:218
